TPU v7x, 32 devices: a whole 2x2x4 slice. The times are simulated.
32 devices in a mesh: groups: 2 (over y), feat: 4 (over x, core), loop: 4 (over z).
Axes of the slice: x: 2, y: 2, z: 4, core: 2. Of those that a mesh axis runs over, the one named last changes fastest.
Arguments:
- train_grads: bfloat16 [512, 65536], P(('groups', 'loop'), 'feat'), parts along dimension 0, may hold values from -6 to 6
- query_grads: bfloat16 [64, 65536], P(('groups', 'loop'), 'feat'), parts along dimension 0, may hold values from -0.0234375 to 0.0234375
- curvature: float32 [65536], P('feat'), may hold values from 0.05 to 5
- row_counts: int32 [8], P(('groups', 'loop')), parts along dimension 0, may hold values from 1 to 64, 128 in all
Outputs:
- scores: float32 [512, 32], P(('groups', 'loop', 'feat')), parts along dimension 0
There are 2 independent parts, one for each index of `groups`. A program takes and returns all parts, laid end to end along the dimension named above; an argument that names none is the same for every part. Nothing has to cross between parts.
Inputs may be any that keep to these rules, and one draw needn't show every extreme that they name: row_counts[s] is the number of live slots of loop shard s; slots 0 to row_counts[s] - 1 of that shard are live; some shard has exactly 64; the counts sum to 128.
All inputs are finite; a program needn't handle non-finite values.
Results may differ from a plain program's by a relative error of at most 0.0029.
Values may be sent and summed in bfloat16 or wider, within the bound.
No kernel may reach another device: no remote copies, remote signals or barrier semaphores. Data moves between devices by JAX's collectives and lax.ppermute only.
A program may use at most 128 MiB of HBM per device.

v0:
```python
import jax
import jax.numpy as jnp
from jax import lax
from jax.sharding import PartitionSpec as P

damping_term = 0.1


def scale_rows(block, curvature):
    return (block.astype(jnp.float32) / (damping_term + curvature[None, :])).astype(jnp.bfloat16)


def product(rows, piece):
    return lax.dot_general(
        rows, piece, (((1,), (1,)), ((), ())), preferred_element_type=jnp.float32
    )


def on_device(train_grads, query_grads, curvature, row_counts):
    slots = train_grads.shape[0]
    live_count = row_counts[0]
    live = (jnp.arange(slots, dtype=jnp.int32) < live_count)[:, None]
    scaled = scale_rows(lax.all_gather(query_grads, "loop", axis=0, tiled=True), curvature)
    raw = product(train_grads, scaled)
    partial_scores = jnp.where(live, raw, jnp.float32(0.0))
    return lax.psum_scatter(partial_scores, "feat", scatter_dimension=0, tiled=True)


def solution(mesh):
    placed = (
        P(("groups", "loop"), "feat"),
        P(("groups", "loop"), "feat"),
        P("feat"),
        P(("groups", "loop")),
    )
    return jax.shard_map(
        on_device,
        mesh=mesh,
        in_specs=placed,
        out_specs=P(("groups", "loop", "feat"), None),
        check_vma=False,
    )
```

profile of v0, /device:TPU:0, one launch (start us, length us, event | category | flops | bytes accessed | tf_op | source)
XLA Modules:
  0.0 68.1 jit_solution(11935903031484605481)
XLA Ops:
  6.5 0.0 copy-start
  6.5 0.0 all-gather.2.cloned.1.call-start
  6.5 0.7 %all-gather.2.cloned.1.call-update = ((bf16[8,16384]{1,0:T(8,128)(2,1)}), bf16[32,16384]{1,0:T(8,128)(2,1)}) async-update(((), (), s32[]{:S(2)}) %all-gather.2.cloned.1.call-start, bf16[8,16384]{1,0:T(8,128)(2,1)} %param.5) | async-update | bytes 1572888
  7.3 0.0 reduce-scatter.4.cloned.1.call-start
  8.0 0.8 %broadcast_add_fusion = f32[16384]{0:T(1024)S(1)} fusion(f32[16384]{0:T(1024)} %param.6), kind=kLoop, calls=%fused_computation.3 | loop fusion | flops 16384 | bytes 131072 | tf_op jit(solution)/shard_map/add | solution.py:10
  8.8 30.8 %all-gather.2.cloned.1.call-done = bf16[32,16384]{1,0:T(8,128)(2,1)} async-done(((bf16[8,16384]{1,0:T(8,128)(2,1)}), bf16[32,16384]{1,0:T(8,128)(2,1)}) %all-gather.2.cloned.1.call-update) | async-done | bytes 1048592 | tf_op jit(solution)/shard_map/all_gather | solution.py:23
  39.6 0.0 copy-done
  39.6 1.9 %fusion = f32[64,32]{0,1:T(8,128)S(1)} fusion(bf16[64,16384]{1,0:T(8,128)(2,1)S(1)} %copy-done, bf16[32,16384]{1,0:T(8,128)(2,1)} %all-gather.2.cloned.1.call-done, f32[16384]{0:T(1024)S(1)} %broadcast_add_fusion, pred[64]{0:T(512)(128)(4,1)S(1)} %iota_compare_fusion), kind=kOutput, calls=%fused_computation.2 | convolution fusion | flops 68683776 | bytes 3219520 | tf_op jit(solution)/shard_map/dot_general | solution.py:14
  41.5 0.7 %copy.7 = f32[64,32]{1,0:T(8,128)} copy(f32[64,32]{0,1:T(8,128)S(1)} %fusion) | data formatting | bytes 16384
  42.2 0.0 reduce-scatter.4.cloned.1.call-update
  42.3 19.0 %reduce-scatter.4.cloned.1.call-done = f32[16,32]{1,0:T(8,128)} async-done(((f32[64,32]{1,0:T(8,128)}), f32[16,32]{1,0:T(8,128)}) %reduce-scatter.4.cloned.1.call-update) | async-done | bytes 2064 | tf_op jit(solution)/shard_map/reduce_scatter | solution.py:26
  (1 shorter events, 0.0 us)
Async XLA Ops:
  6.5 33.1 %copy-start = (bf16[64,16384]{1,0:T(8,128)(2,1)S(1)}, bf16[64,16384]{1,0:T(8,128)(2,1)}, u32[]{:S(2)}) copy-start(bf16[64,16384]{1,0:T(8,128)(2,1)} %param.4) | copy-start | bytes 6291460
  6.5 33.1 %all-gather.2.cloned.1.call-start = ((), (), s32[]{:S(2)}) async-start(), calls=%async_computation.1 | async-start | bytes 1310720 | tf_op jit(solution)/shard_map/all_gather | solution.py:23
  7.3 54.0 %reduce-scatter.4.cloned.1.call-start = ((), (), s32[]{:S(2)}) async-start(), calls=%async_computation.2 | async-start | bytes 40960 | tf_op jit(solution)/shard_map/reduce_scatter | solution.py:26
Sparse Core Ops, SparseCore 0:
  8.9 30.6 all-gather.1
  42.4 18.8 reduce-scatter.3
where the time goes:
time: 68.3 us; the launch traced here: 68.1 us
  waiting for transfers between devices  50.6 us (74%)
  between operations  14.1 us (21%)
  matrix products  1.88 us (3%)
  other arithmetic  0.86 us (1%)
  local copies, waits for them, and re-layouts  0.7 us (1%)
    all_gather x1, waiting for transfers between devices, on_device(): lax.all_gather(query_grads, 'loop', axis=0, tiled=True)  30.8 us
    reduce_scatter x1, waiting for transfers between devices, on_device(): lax.psum_scatter(partial_scores, 'feat', scatter_dimension=0, tiled=True)  19 us
    dot_general x1, matrix products, product(): lax.dot_general(rows, piece, (((1,), (1,)), ((), ())), preferred_element_...  1.88 us
  transfers between devices with their start and end apart: 2, of which 2 were waited for; matrix products, arithmetic and copies ran while one was open for 1% of the time, Pallas kernels for 0%

commit v1 on v0

v1 whole, which is shorter than its diff:
```python
import functools

import jax
import jax.numpy as jnp
from jax import lax
from jax.experimental import pallas as pl
from jax.experimental.pallas import tpu as pltpu
from jax.sharding import PartitionSpec as P

damping_term = 0.1


def scale_rows(block, curvature):
    return (block.astype(jnp.float32) / (damping_term + curvature)).astype(jnp.bfloat16)


def product(rows, piece):
    return lax.dot_general(
        rows, piece, (((1,), (1,)), ((), ())), preferred_element_type=jnp.float32
    )


def gathered(train_grads, query_grads, curvature, row_counts):
    slots = train_grads.shape[0]
    live = (jnp.arange(slots, dtype=jnp.int32) < row_counts[0])[:, None]
    queries = lax.all_gather(query_grads, "loop", axis=0, tiled=True)
    raw = product(train_grads, scale_rows(queries, curvature[None, :]))
    partial_scores = jnp.where(live, raw, jnp.float32(0.0))
    return lax.psum_scatter(partial_scores, "feat", scatter_dimension=0, tiled=True)


def score_kernel(shards, where_ref, count_ref, train_ref, curve_ref, *refs):
    pieces, outs, acc_t, acc = refs[: shards + 2], refs[shards + 2 : -2], refs[-2], refs[-1]
    me, part = where_ref[0], where_ref[1]
    damp = damping_term + curve_ref[...]
    train = train_ref[...]
    for hop in range(shards):
        rows = pieces[hop][...].astype(jnp.float32)
        if hop >= 2:
            rows = rows + pieces[hop + 2][...].astype(jnp.float32)
        scaled = (rows / damp).astype(jnp.bfloat16)
        acc_t[me ^ hop] = product(scaled, train)
    slots = train_ref.shape[0]
    table = acc_t[...].reshape(-1, slots).T
    live = lax.broadcasted_iota(jnp.int32, table.shape, 0) < count_ref[0]
    acc[...] = jnp.where(live, table, 0.0)
    height = outs[0].shape[0]
    for hop, out in enumerate(outs):
        out[...] = acc[pl.ds(pl.multiple_of((part ^ hop) * height, height), height), :]


def permuted(n_feat, train_grads, query_grads, curvature, row_counts):
    swap = lambda pairs: lax.ppermute(query_grads, "loop", pairs)
    far_in = swap([(0, 2), (3, 1)])
    near = swap([(0, 1), (1, 0), (2, 3), (3, 2)])
    far_out = swap([(1, 3), (2, 0)])
    middle = swap([(1, 2), (2, 1)])
    passed = lax.ppermute(far_in, "loop", [(2, 3), (1, 0)])
    me, part = lax.axis_index("loop"), lax.axis_index("feat")
    pieces = (query_grads, near, far_in, middle, far_out, passed)
    slots, features = train_grads.shape
    rows = query_grads.shape[0]
    queries = 4 * rows
    vmem = pl.BlockSpec(memory_space=pltpu.VMEM)
    smem = pl.BlockSpec(memory_space=pltpu.SMEM)
    block = jax.ShapeDtypeStruct((slots // n_feat, queries), jnp.float32)
    blocks = pl.pallas_call(
        functools.partial(score_kernel, 4),
        out_shape=[block] * n_feat,
        in_specs=[smem, smem] + [vmem] * (2 + len(pieces)),
        out_specs=[vmem] * n_feat,
        scratch_shapes=[
            pltpu.VMEM((4, rows, slots), jnp.float32),
            pltpu.VMEM((slots, queries), jnp.float32),
        ],
        compiler_params=pltpu.CompilerParams(vmem_limit_bytes=16 << 20),
        name="score",
    )(jnp.stack([me, part]), row_counts, train_grads, curvature[None, :], *pieces)
    total = blocks[0]
    for hop in range(1, n_feat):
        total = total + lax.ppermute(blocks[hop], "feat", [(i, i ^ hop) for i in range(n_feat)])
    return total


def solution(mesh):
    placed = (
        P(("groups", "loop"), "feat"),
        P(("groups", "loop"), "feat"),
        P("feat"),
        P(("groups", "loop")),
    )
    n_loop, n_feat = mesh.shape["loop"], mesh.shape["feat"]
    body = functools.partial(permuted, n_feat) if n_loop == 4 and n_feat & (n_feat - 1) == 0 else gathered
    return jax.shard_map(
        body,
        mesh=mesh,
        in_specs=placed,
        out_specs=P(("groups", "loop", "feat"), None),
        check_vma=False,
    )
```

time: 68.3 us -> 38.8 us (0.57)
  waiting for transfers between devices: 50.6 us -> 18.5 us
  between operations: 14.1 us -> 0.71 us
  starting transfers between devices: 0.04 us -> 12.4 us
  Pallas kernels: 0 us -> 2.9 us
  local copies, waits for them, and re-layouts: 0.7 us -> 3.38 us
  matrix products: 1.88 us -> 0 us
    all_gather x1 -> x0, waiting for transfers between devices: 30.8 us -> none  [on_device(): lax.all_gather(query_grads, 'loop', axis=0, tiled=True)]
    reduce_scatter x1 -> x0, waiting for transfers between devices: 19 us -> none  [on_device(): lax.psum_scatter(partial_scores, 'feat', scatter_dimension=0, tiled=True)]
    ppermute x0 -> x8, waiting for transfers between devices: none -> 18.5 us  [the longest x4 13.7 us: permuted(): swap = lambda pairs: lax.ppermute(query_grads, 'loop', pairs)]
    ppermute x0 -> x8, starting transfers between devices: none -> 12.4 us  [the longest x4 9.16 us: permuted(): swap = lambda pairs: lax.ppermute(query_grads, 'loop', pairs)]
    pallas_call x0 -> x1, Pallas kernels: none -> 2.9 us  [permuted(): pl.pallas_call(functools.partial(score_kernel, 4), out_shape=[block] * n_...]
    unnamed x3 -> x6, local copies, waits for them, and re-layouts: 0.7 us -> 3.38 us
    dot_general x1 -> x0, matrix products: 1.88 us -> none  [product(): lax.dot_general(rows, piece, (((1,), (1,)), ((), ())), preferred_element_...]
    unnamed x2 -> x0, waiting for transfers between devices: 0.73 us -> none
  transfers between devices with their start and end apart: 2 -> 8, of which waited for: 2 -> 6; matrix products, arithmetic and copies ran while one was open for 1% -> 0% of each run, Pallas kernels for 0% -> 0%
where the time goes in v1:
time: 38.8 us; the launch traced here: 38.5 us
  waiting for transfers between devices  18.5 us (48%)
  starting transfers between devices  12.4 us (32%)
  local copies, waits for them, and re-layouts  3.38 us (9%)
  Pallas kernels  2.9 us (7%)
  between operations  0.71 us (2%)
  other arithmetic  0.68 us (2%)
    ppermute x4, waiting for transfers between devices, permuted(): swap = lambda pairs: lax.ppermute(query_grads, 'loop', pairs)  13.7 us
    ppermute x4, starting transfers between devices, permuted(): swap = lambda pairs: lax.ppermute(query_grads, 'loop', pairs)  9.16 us
    unnamed x6, local copies, waits for them, and re-layouts  3.38 us
    pallas_call x1, Pallas kernels, permuted(): pl.pallas_call(functools.partial(score_kernel, 4), out_shape=[block] * n_...  2.9 us
    ppermute x3, waiting for transfers between devices, permuted(): lax.ppermute(blocks[hop], 'feat', [(i, i ^ hop) for i in range(n_feat)])  2.78 us
    ppermute x1, waiting for transfers between devices, permuted(): passed = lax.ppermute(far_in, 'loop', [(2, 3), (1, 0)])  2.01 us
    ppermute x3, starting transfers between devices, permuted(): lax.ppermute(blocks[hop], 'feat', [(i, i ^ hop) for i in range(n_feat)])  1.92 us
    ppermute x1, starting transfers between devices, permuted(): passed = lax.ppermute(far_in, 'loop', [(2, 3), (1, 0)])  1.28 us
  transfers between devices with their start and end apart: 8, of which 6 were waited for; matrix products, arithmetic and copies ran while one was open for 0% of the time, Pallas kernels for 0%

profile of v1, /device:TPU:0, one launch (start us, length us, event | category | flops | bytes accessed | tf_op | source)
XLA Modules:
  0.0 38.5 jit_solution(9491846756276592117)
XLA Ops:
  0.0 6.0 %collective-permute-start.1 = (bf16[8,16384]{1,0:T(8,128)(2,1)}, bf16[8,16384]{1,0:T(8,128)(2,1)S(1)}, u32[]{:S(2)}, u32[]{:S(2)}) collective-permute-start(bf16[8,16384]{1,0:T(8,128)(2,1)} %refs_0_.1), channel_id=1, source_target_pairs={{0,2},{3,1},{4,6},{7,5},{8,10},{11,9},{12,14},{15,13},{16,18},{19,... | collective-permute-start | bytes 786440 | tf_op jit(solution)/shard_map/ppermute | solution.py:53
  6.0 0.7 %collective-permute-start.2 = (bf16[8,16384]{1,0:T(8,128)(2,1)}, bf16[8,16384]{1,0:T(8,128)(2,1)S(1)}, u32[]{:S(2)}, u32[]{:S(2)}) collective-permute-start(bf16[8,16384]{1,0:T(8,128)(2,1)} %refs_0_.1), channel_id=1, source_target_pairs={{1,2},{2,1},{5,6},{6,5},{9,10},{10,9},{13,14},{14,13},{17,18},{18,... | collective-permute-start | bytes 786440 | tf_op jit(solution)/shard_map/ppermute | solution.py:53
  6.7 1.2 %collective-permute-start = (bf16[8,16384]{1,0:T(8,128)(2,1)}, bf16[8,16384]{1,0:T(8,128)(2,1)S(1)}, u32[]{:S(2)}, u32[]{:S(2)}) collective-permute-start(bf16[8,16384]{1,0:T(8,128)(2,1)} %refs_0_.1), channel_id=1, source_target_pairs={{0,1},{1,0},{2,3},{3,2},{4,5},{5,4},{6,7},{7,6},{8,9},{9,8},{10,11... | collective-permute-start | bytes 786440 | tf_op jit(solution)/shard_map/ppermute | solution.py:53
  7.9 1.3 %collective-permute-start.3 = (bf16[8,16384]{1,0:T(8,128)(2,1)}, bf16[8,16384]{1,0:T(8,128)(2,1)S(1)}, u32[]{:S(2)}, u32[]{:S(2)}) collective-permute-start(bf16[8,16384]{1,0:T(8,128)(2,1)} %refs_0_.1), channel_id=1, source_target_pairs={{1,3},{2,0},{5,7},{6,4},{9,11},{10,8},{13,15},{14,12},{17,19},{18,... | collective-permute-start | bytes 786440 | tf_op jit(solution)/shard_map/ppermute | solution.py:53
  9.2 3.8 %collective-permute-done.1.refs_2_ = bf16[8,16384]{1,0:T(8,128)(2,1)S(1)} collective-permute-done((bf16[8,16384]{1,0:T(8,128)(2,1)}, bf16[8,16384]{1,0:T(8,128)(2,1)S(1)}, u32[]{:S(2)}, u32[]{:S(2)}) %collective-permute-start.1) | collective-permute-done | bytes 262176 | tf_op jit(solution)/shard_map/ppermute | solution.py:53
  13.0 1.3 %collective-permute-start.4 = (bf16[8,16384]{1,0:T(8,128)(2,1)S(1)}, bf16[8,16384]{1,0:T(8,128)(2,1)S(1)}, u32[]{:S(2)}, u32[]{:S(2)}) collective-permute-start(bf16[8,16384]{1,0:T(8,128)(2,1)S(1)} %collective-permute-done.1.refs_2_), channel_id=1, source_target_pairs={{2,3},{1,0},{6,7},{5,4},{10,11},{9,8},{14,15},{13,12},{18,19},{17,... | collective-permute-start | bytes 786440 | tf_op jit(solution)/shard_map/ppermute | solution.py:58
  14.9 0.1 pad_add_fusion.where_ref
  15.0 0.0 collective-permute-done.2.refs_3_
  15.0 2.5 %collective-permute-done.refs_1_ = bf16[8,16384]{1,0:T(8,128)(2,1)S(1)} collective-permute-done((bf16[8,16384]{1,0:T(8,128)(2,1)}, bf16[8,16384]{1,0:T(8,128)(2,1)S(1)}, u32[]{:S(2)}, u32[]{:S(2)}) %collective-permute-start) | collective-permute-done | bytes 262176 | tf_op jit(solution)/shard_map/ppermute | solution.py:53
  17.5 7.4 %collective-permute-done.3.refs_4_ = bf16[8,16384]{1,0:T(8,128)(2,1)S(1)} collective-permute-done((bf16[8,16384]{1,0:T(8,128)(2,1)}, bf16[8,16384]{1,0:T(8,128)(2,1)S(1)}, u32[]{:S(2)}, u32[]{:S(2)}) %collective-permute-start.3) | collective-permute-done | bytes 262176 | tf_op jit(solution)/shard_map/ppermute | solution.py:53
  24.9 2.0 %collective-permute-done.4.refs_5_ = bf16[8,16384]{1,0:T(8,128)(2,1)S(1)} collective-permute-done((bf16[8,16384]{1,0:T(8,128)(2,1)S(1)}, bf16[8,16384]{1,0:T(8,128)(2,1)S(1)}, u32[]{:S(2)}, u32[]{:S(2)}) %collective-permute-start.4) | collective-permute-done | bytes 262176 | tf_op jit(solution)/shard_map/ppermute | solution.py:58
  26.9 0.0 copy-start
  26.9 1.6 %copy-done = bf16[64,16384]{1,0:T(8,128)(2,1)S(1)} copy-done((bf16[64,16384]{1,0:T(8,128)(2,1)S(1)}, bf16[64,16384]{1,0:T(8,128)(2,1)}, u32[]{:S(2)}) %copy-start) | copy-done | bytes 2097176
  28.5 0.0 copy-start.1
  28.5 0.9 %copy-done.1 = bf16[8,16384]{1,0:T(8,128)(2,1)S(1)} copy-done((bf16[8,16384]{1,0:T(8,128)(2,1)S(1)}, bf16[8,16384]{1,0:T(8,128)(2,1)}, u32[]{:S(2)}) %copy-start.1) | copy-done | bytes 262168
  29.4 0.0 copy-start.2
  29.4 0.8 %copy-done.2 = f32[16384]{0:T(1024)S(1)} copy-done((f32[16384]{0:T(1024)S(1)}, f32[16384]{0:T(1024)}, u32[]{:S(2)}) %copy-start.2) | copy-done | bytes 65560
  30.3 2.9 %score.1 = (f32[16,32]{1,0:T(8,128)S(1)}, f32[16,32]{1,0:T(8,128)S(1)}, f32[16,32]{1,0:T(8,128)S(1)}, f32[16,32]{1,0:T(8,128)S(1)}) custom-call(s32[2]{0:T(128)S(1)} %pad_add_fusion.where_ref, s32[1]{0:T(128)S(6)} %copy.5.count_ref, bf16[64,16384]{1,0:T(8,128)(2,1)S(1)} %copy-done, f32[1,16384]{1,0:T(1,128)S(1)} %bitcast.3, bf16[8,16384]{1,0:T(8,128)(2,1)S(1)} %copy-done.1, ...), custom_call_target="tpu_custom_call" | custom-call | tf_op jit(solution)/shard_map/score/pallas_call | solution.py:67
  33.2 0.1 collective-permute-start.5
  33.2 1.6 %collective-permute-start.6 = (f32[16,32]{1,0:T(8,128)S(1)}, f32[16,32]{1,0:T(8,128)S(1)}, u32[]{:S(2)}, u32[]{:S(2)}) collective-permute-start(f32[16,32]{1,0:T(8,128)S(1)} %get-tuple-element.11), channel_id=1, source_target_pairs={{0,8},{4,12},{8,0},{12,4},{1,9},{5,13},{9,1},{13,5},{2,10},{6,14},... | collective-permute-start | bytes 6152 | tf_op jit(solution)/shard_map/ppermute | solution.py:81
  34.8 0.3 collective-permute-start.7
  35.1 0.0 collective-permute-done.5
  35.1 1.9 %collective-permute-done.6 = f32[16,32]{1,0:T(8,128)S(1)} collective-permute-done((f32[16,32]{1,0:T(8,128)S(1)}, f32[16,32]{1,0:T(8,128)S(1)}, u32[]{:S(2)}, u32[]{:S(2)}) %collective-permute-start.6) | collective-permute-done | bytes 2080 | tf_op jit(solution)/shard_map/ppermute | solution.py:81
  37.0 0.9 %collective-permute-done.7 = f32[16,32]{1,0:T(8,128)S(1)} collective-permute-done((f32[16,32]{1,0:T(8,128)S(1)}, f32[16,32]{1,0:T(8,128)S(1)}, u32[]{:S(2)}, u32[]{:S(2)}) %collective-permute-start.7) | collective-permute-done | bytes 2080 | tf_op jit(solution)/shard_map/ppermute | solution.py:81
  37.9 0.6 %add_add_fusion = f32[16,32]{1,0:T(8,128)} fusion(f32[16,32]{1,0:T(8,128)S(1)} %collective-permute-done.7, f32[16,32]{1,0:T(8,128)S(1)} %collective-permute-done.6, f32[16,32]{1,0:T(8,128)S(1)} %get-tuple-element.9, f32[16,32]{1,0:T(8,128)S(1)} %collective-permute-done.5), kind=kLoop, calls=%fused_computation | loop fusion | flops 1536 | bytes 10240 | tf_op jit(solution)/shard_map/add | solution.py:81
Async XLA Ops:
  0.0 13.0 %collective-permute-start.1 = (bf16[8,16384]{1,0:T(8,128)(2,1)}, bf16[8,16384]{1,0:T(8,128)(2,1)S(1)}, u32[]{:S(2)}, u32[]{:S(2)}) collective-permute-start(bf16[8,16384]{1,0:T(8,128)(2,1)} %refs_0_.1), channel_id=1, source_target_pairs={{0,2},{3,1},{4,6},{7,5},{8,10},{11,9},{12,14},{15,13},{16,18},{19,... | collective-permute-start | bytes 786440 | tf_op jit(solution)/shard_map/ppermute | solution.py:53
  6.0 9.0 %collective-permute-start.2 = (bf16[8,16384]{1,0:T(8,128)(2,1)}, bf16[8,16384]{1,0:T(8,128)(2,1)S(1)}, u32[]{:S(2)}, u32[]{:S(2)}) collective-permute-start(bf16[8,16384]{1,0:T(8,128)(2,1)} %refs_0_.1), channel_id=1, source_target_pairs={{1,2},{2,1},{5,6},{6,5},{9,10},{10,9},{13,14},{14,13},{17,18},{18,... | collective-permute-start | bytes 786440 | tf_op jit(solution)/shard_map/ppermute | solution.py:53
  6.7 10.8 %collective-permute-start = (bf16[8,16384]{1,0:T(8,128)(2,1)}, bf16[8,16384]{1,0:T(8,128)(2,1)S(1)}, u32[]{:S(2)}, u32[]{:S(2)}) collective-permute-start(bf16[8,16384]{1,0:T(8,128)(2,1)} %refs_0_.1), channel_id=1, source_target_pairs={{0,1},{1,0},{2,3},{3,2},{4,5},{5,4},{6,7},{7,6},{8,9},{9,8},{10,11... | collective-permute-start | bytes 786440 | tf_op jit(solution)/shard_map/ppermute | solution.py:53
  7.9 17.0 %collective-permute-start.3 = (bf16[8,16384]{1,0:T(8,128)(2,1)}, bf16[8,16384]{1,0:T(8,128)(2,1)S(1)}, u32[]{:S(2)}, u32[]{:S(2)}) collective-permute-start(bf16[8,16384]{1,0:T(8,128)(2,1)} %refs_0_.1), channel_id=1, source_target_pairs={{1,3},{2,0},{5,7},{6,4},{9,11},{10,8},{13,15},{14,12},{17,19},{18,... | collective-permute-start | bytes 786440 | tf_op jit(solution)/shard_map/ppermute | solution.py:53
  13.0 13.9 %collective-permute-start.4 = (bf16[8,16384]{1,0:T(8,128)(2,1)S(1)}, bf16[8,16384]{1,0:T(8,128)(2,1)S(1)}, u32[]{:S(2)}, u32[]{:S(2)}) collective-permute-start(bf16[8,16384]{1,0:T(8,128)(2,1)S(1)} %collective-permute-done.1.refs_2_), channel_id=1, source_target_pairs={{2,3},{1,0},{6,7},{5,4},{10,11},{9,8},{14,15},{13,12},{18,19},{17,... | collective-permute-start | bytes 786440 | tf_op jit(solution)/shard_map/ppermute | solution.py:58
  26.9 1.6 %copy-start = (bf16[64,16384]{1,0:T(8,128)(2,1)S(1)}, bf16[64,16384]{1,0:T(8,128)(2,1)}, u32[]{:S(2)}) copy-start(bf16[64,16384]{1,0:T(8,128)(2,1)} %train_ref.1) | copy-start | bytes 6291460
  28.5 0.9 %copy-start.1 = (bf16[8,16384]{1,0:T(8,128)(2,1)S(1)}, bf16[8,16384]{1,0:T(8,128)(2,1)}, u32[]{:S(2)}) copy-start(bf16[8,16384]{1,0:T(8,128)(2,1)} %refs_0_.1) | copy-start | bytes 786436
  29.4 0.8 %copy-start.2 = (f32[16384]{0:T(1024)S(1)}, f32[16384]{0:T(1024)}, u32[]{:S(2)}) copy-start(f32[16384]{0:T(1024)} %param.6) | copy-start | bytes 196612
  33.2 1.9 %collective-permute-start.5 = (f32[16,32]{1,0:T(8,128)S(1)}, f32[16,32]{1,0:T(8,128)S(1)}, u32[]{:S(2)}, u32[]{:S(2)}) collective-permute-start(f32[16,32]{1,0:T(8,128)S(1)} %get-tuple-element.10), channel_id=1, source_target_pairs={{0,4},{4,0},{8,12},{12,8},{1,5},{5,1},{9,13},{13,9},{2,6},{6,2},{1... | collective-permute-start | bytes 6152 | tf_op jit(solution)/shard_map/ppermute | solution.py:81
  33.2 3.7 %collective-permute-start.6 = (f32[16,32]{1,0:T(8,128)S(1)}, f32[16,32]{1,0:T(8,128)S(1)}, u32[]{:S(2)}, u32[]{:S(2)}) collective-permute-start(f32[16,32]{1,0:T(8,128)S(1)} %get-tuple-element.11), channel_id=1, source_target_pairs={{0,8},{4,12},{8,0},{12,4},{1,9},{5,13},{9,1},{13,5},{2,10},{6,14},... | collective-permute-start | bytes 6152 | tf_op jit(solution)/shard_map/ppermute | solution.py:81
  34.8 3.1 %collective-permute-start.7 = (f32[16,32]{1,0:T(8,128)S(1)}, f32[16,32]{1,0:T(8,128)S(1)}, u32[]{:S(2)}, u32[]{:S(2)}) collective-permute-start(f32[16,32]{1,0:T(8,128)S(1)} %get-tuple-element.12), channel_id=1, source_target_pairs={{0,12},{4,8},{8,4},{12,0},{1,13},{5,9},{9,5},{13,1},{2,14},{6,10},... | collective-permute-start | bytes 6152 | tf_op jit(solution)/shard_map/ppermute | solution.py:81

commit v2 on v0

v2 whole, which is shorter than its diff:
```python
import functools

import jax
import jax.numpy as jnp
from jax import lax
from jax.experimental import pallas as pl
from jax.experimental.pallas import tpu as pltpu
from jax.sharding import PartitionSpec as P

damping_term = 0.1
vmem = pl.BlockSpec(memory_space=pltpu.VMEM)
smem = pl.BlockSpec(memory_space=pltpu.SMEM)
grant = pltpu.CompilerParams(vmem_limit_bytes=16 << 20)


def product(rows, piece):
    return lax.dot_general(
        rows, piece, (((1,), (1,)), ((), ())), preferred_element_type=jnp.float32
    )


def gathered(train_grads, query_grads, curvature, row_counts):
    slots = train_grads.shape[0]
    live = (jnp.arange(slots, dtype=jnp.int32) < row_counts[0])[:, None]
    queries = lax.all_gather(query_grads, "loop", axis=0, tiled=True).astype(jnp.float32)
    scaled = (queries / (damping_term + curvature[None, :])).astype(jnp.bfloat16)
    partial_scores = jnp.where(live, product(train_grads, scaled), jnp.float32(0.0))
    return lax.psum_scatter(partial_scores, "feat", scatter_dimension=0, tiled=True)


def own_kernel(train_ref, curve_ref, own_ref, score_ref, gain_ref):
    gain_ref[...] = 1.0 / (damping_term + curve_ref[...])
    own = own_ref[...]
    scaled = (own.astype(jnp.float32) * gain_ref[...]).astype(jnp.bfloat16)
    score_ref[...] = product(scaled, train_ref[...])


def early_kernel(train_ref, gain_ref, near_ref, far_ref, near_score, far_score):
    gain = gain_ref[...]
    near = near_ref[...].astype(jnp.float32) * gain
    near_score[...] = product(near.astype(jnp.bfloat16), train_ref[...])
    far = far_ref[...].astype(jnp.float32) * gain
    far_score[...] = product(far.astype(jnp.bfloat16), train_ref[...])


def last_kernel(where_ref, count_ref, train_ref, gain_ref, own, near, far, cross, *refs):
    outs, table, scores = refs[:-2], refs[-2], refs[-1]
    me, part = where_ref[0], where_ref[1]
    last = cross[...].astype(jnp.float32) * gain_ref[...]
    table[me] = own[...]
    table[me ^ 1] = near[...]
    table[me ^ 2] = far[...]
    table[me ^ 3] = product(last.astype(jnp.bfloat16), train_ref[...])
    slots = train_ref.shape[0]
    whole = table[...].reshape(-1, slots).T
    live = lax.broadcasted_iota(jnp.int32, whole.shape, 0) < count_ref[0]
    scores[...] = jnp.where(live, whole, 0.0)
    height = outs[0].shape[0]
    for hop, out in enumerate(outs):
        out[...] = scores[pl.ds(pl.multiple_of((part ^ hop) * height, height), height), :]


def permuted(n_feat, train_grads, query_grads, curvature, row_counts):
    slots, features = train_grads.shape
    rows = query_grads.shape[0]
    def send(piece, pairs):
        return lax.ppermute(piece, "loop", pairs)
    score = jax.ShapeDtypeStruct((rows, slots), jnp.float32)
    far = send(query_grads, [(i, i ^ 2) for i in range(4)])
    near = send(query_grads, [(i, i ^ 1) for i in range(4)])
    own_score, gain = pl.pallas_call(
        own_kernel,
        out_shape=[score, jax.ShapeDtypeStruct((1, features), jnp.float32)],
        in_specs=[vmem] * 3,
        out_specs=[vmem] * 2,
        compiler_params=grant,
        name="own",
    )(train_grads, curvature[None, :], query_grads)
    cross = send(far, [(i, i ^ 1) for i in range(4)])
    near_score, far_score = pl.pallas_call(
        early_kernel,
        out_shape=[score] * 2,
        in_specs=[vmem] * 4,
        out_specs=[vmem] * 2,
        compiler_params=grant,
        name="early",
    )(train_grads, gain, near, far)
    place = jnp.stack([lax.axis_index("loop"), lax.axis_index("feat")])
    block = jax.ShapeDtypeStruct((slots // n_feat, 4 * rows), jnp.float32)
    blocks = pl.pallas_call(
        last_kernel,
        out_shape=[block] * n_feat,
        in_specs=[smem] * 2 + [vmem] * 6,
        out_specs=[vmem] * n_feat,
        scratch_shapes=[
            pltpu.VMEM((4, rows, slots), jnp.float32),
            pltpu.VMEM((slots, 4 * rows), jnp.float32),
        ],
        compiler_params=grant,
        name="last",
    )(place, row_counts, train_grads, gain, own_score, near_score, far_score, cross)
    total = blocks[0]
    for hop in range(1, n_feat):
        total = total + lax.ppermute(blocks[hop], "feat", [(i, i ^ hop) for i in range(n_feat)])
    return total


def solution(mesh):
    placed = (
        P(("groups", "loop"), "feat"),
        P(("groups", "loop"), "feat"),
        P("feat"),
        P(("groups", "loop")),
    )
    n_loop, n_feat = mesh.shape["loop"], mesh.shape["feat"]
    short = n_loop == 4 and n_feat & (n_feat - 1) == 0
    return jax.shard_map(
        functools.partial(permuted, n_feat) if short else gathered,
        mesh=mesh,
        in_specs=placed,
        out_specs=P(("groups", "loop", "feat"), None),
        check_vma=False,
    )
```

time: 68.3 us -> 30.3 us (0.44)
  waiting for transfers between devices: 50.6 us -> 14 us
  between operations: 14.1 us -> 0.68 us
  starting transfers between devices: 0.04 us -> 8.29 us
  Pallas kernels: 0 us -> 3.12 us
  local copies, waits for them, and re-layouts: 0.7 us -> 3.37 us
  matrix products: 1.88 us -> 0 us
    all_gather x1 -> x0, waiting for transfers between devices: 30.8 us -> none  [on_device(): lax.all_gather(query_grads, 'loop', axis=0, tiled=True)]
    reduce_scatter x1 -> x0, waiting for transfers between devices: 19 us -> none  [on_device(): lax.psum_scatter(partial_scores, 'feat', scatter_dimension=0, tiled=True)]
    ppermute x0 -> x6, waiting for transfers between devices: none -> 14 us  [the longest x3 11.4 us: send(): return lax.ppermute(piece, 'loop', pairs)]
    ppermute x0 -> x6, starting transfers between devices: none -> 8.29 us  [the longest x3 6.37 us: send(): return lax.ppermute(piece, 'loop', pairs)]
    pallas_call x0 -> x3, Pallas kernels: none -> 3.12 us  [the longest x1 1.28 us: permuted(): pl.pallas_call(last_kernel, out_shape=[block] * n_feat, in_specs=[smem] *...]
    unnamed x3 -> x6, local copies, waits for them, and re-layouts: 0.7 us -> 3.37 us
    dot_general x1 -> x0, matrix products: 1.88 us -> none  [product(): lax.dot_general(rows, piece, (((1,), (1,)), ((), ())), preferred_element_...]
    unnamed x2 -> x0, waiting for transfers between devices: 0.73 us -> none
  transfers between devices with their start and end apart: 2 -> 6, of which waited for: 2 -> 4; matrix products, arithmetic and copies ran while one was open for 1% -> 0% of each run, Pallas kernels for 0% -> 6%
where the time goes in v2:
time: 30.3 us; the launch traced here: 30.1 us
  waiting for transfers between devices  14 us (46%)
  starting transfers between devices  8.29 us (27%)
  local copies, waits for them, and re-layouts  3.37 us (11%)
  Pallas kernels  3.12 us (10%)
  other arithmetic  0.68 us (2%)
  between operations  0.68 us (2%)
    ppermute x3, waiting for transfers between devices, send(): return lax.ppermute(piece, 'loop', pairs)  11.4 us
    ppermute x3, starting transfers between devices, send(): return lax.ppermute(piece, 'loop', pairs)  6.37 us
    unnamed x6, local copies, waits for them, and re-layouts  3.37 us
    ppermute x3, waiting for transfers between devices, permuted(): lax.ppermute(blocks[hop], 'feat', [(i, i ^ hop) for i in range(n_feat)])  2.58 us
    ppermute x3, starting transfers between devices, permuted(): lax.ppermute(blocks[hop], 'feat', [(i, i ^ hop) for i in range(n_feat)])  1.92 us
    pallas_call x1, Pallas kernels, permuted(): pl.pallas_call(last_kernel, out_shape=[block] * n_feat, in_specs=[smem] *...  1.28 us
    pallas_call x1, Pallas kernels, permuted(): pl.pallas_call(early_kernel, out_shape=[score] * 2, in_specs=[vmem] * 4,...  1.19 us
    pallas_call x1, Pallas kernels, permuted(): pl.pallas_call(own_kernel, out_shape=[score, jax.ShapeDtypeStruct((1, fea...  0.64 us
  transfers between devices with their start and end apart: 6, of which 4 were waited for; matrix products, arithmetic and copies ran while one was open for 0% of the time, Pallas kernels for 6%

profile of v2, /device:TPU:0, one launch (start us, length us, event | category | flops | bytes accessed | tf_op | source)
XLA Modules:
  0.0 30.1 jit_solution(5130861343504216272)
XLA Ops:
  0.0 4.1 %collective-permute-start.1 = (bf16[8,16384]{1,0:T(8,128)(2,1)}, bf16[8,16384]{1,0:T(8,128)(2,1)S(1)}, u32[]{:S(2)}, u32[]{:S(2)}) collective-permute-start(bf16[8,16384]{1,0:T(8,128)(2,1)} %own_ref.1), channel_id=1, source_target_pairs={{0,2},{1,3},{2,0},{3,1},{4,6},{5,7},{6,4},{7,5},{8,10},{9,11},{10,... | collective-permute-start | bytes 786440 | tf_op jit(solution)/shard_map/ppermute | solution.py:67
  4.1 1.6 %collective-permute-start = (bf16[8,16384]{1,0:T(8,128)(2,1)}, bf16[8,16384]{1,0:T(8,128)(2,1)S(1)}, u32[]{:S(2)}, u32[]{:S(2)}) collective-permute-start(bf16[8,16384]{1,0:T(8,128)(2,1)} %own_ref.1), channel_id=1, source_target_pairs={{0,1},{1,0},{2,3},{3,2},{4,5},{5,4},{6,7},{7,6},{8,9},{9,8},{10,11... | collective-permute-start | bytes 786440 | tf_op jit(solution)/shard_map/ppermute | solution.py:67
  5.6 10.7 %collective-permute-done.1.far_ref = bf16[8,16384]{1,0:T(8,128)(2,1)S(1)} collective-permute-done((bf16[8,16384]{1,0:T(8,128)(2,1)}, bf16[8,16384]{1,0:T(8,128)(2,1)S(1)}, u32[]{:S(2)}, u32[]{:S(2)}) %collective-permute-start.1) | collective-permute-done | bytes 262176 | tf_op jit(solution)/shard_map/ppermute | solution.py:67
  16.3 0.7 %collective-permute-start.2 = (bf16[8,16384]{1,0:T(8,128)(2,1)S(1)}, bf16[8,16384]{1,0:T(8,128)(2,1)S(1)}, u32[]{:S(2)}, u32[]{:S(2)}) collective-permute-start(bf16[8,16384]{1,0:T(8,128)(2,1)S(1)} %collective-permute-done.1.far_ref), channel_id=1, source_target_pairs={{0,1},{1,0},{2,3},{3,2},{4,5},{5,4},{6,7},{7,6},{8,9},{9,8},{10,11... | collective-permute-start | bytes 786440 | tf_op jit(solution)/shard_map/ppermute | solution.py:67
  17.7 0.0 copy-start
  17.7 1.6 %copy-done = bf16[64,16384]{1,0:T(8,128)(2,1)S(1)} copy-done((bf16[64,16384]{1,0:T(8,128)(2,1)S(1)}, bf16[64,16384]{1,0:T(8,128)(2,1)}, u32[]{:S(2)}) %copy-start) | copy-done | bytes 2097176
  19.3 0.0 copy-start.1
  19.3 0.9 %copy-done.1 = bf16[8,16384]{1,0:T(8,128)(2,1)S(1)} copy-done((bf16[8,16384]{1,0:T(8,128)(2,1)S(1)}, bf16[8,16384]{1,0:T(8,128)(2,1)}, u32[]{:S(2)}) %copy-start.1) | copy-done | bytes 262168
  20.2 0.0 copy-start.2
  20.2 0.8 %copy-done.2 = f32[16384]{0:T(1024)S(1)} copy-done((f32[16384]{0:T(1024)S(1)}, f32[16384]{0:T(1024)}, u32[]{:S(2)}) %copy-start.2) | copy-done | bytes 65560
  21.1 0.6 %own.1 = (f32[8,64]{1,0:T(8,128)S(1)}, f32[1,16384]{1,0:T(1,128)S(1)}) custom-call(bf16[64,16384]{1,0:T(8,128)(2,1)S(1)} %copy-done, f32[1,16384]{1,0:T(1,128)S(1)} %bitcast.3, bf16[8,16384]{1,0:T(8,128)(2,1)S(1)} %copy-done.1), custom_call_target="tpu_custom_call" | custom-call | tf_op jit(solution)/shard_map/own/pallas_call | solution.py:71
  21.7 0.1 pad_add_fusion.where_ref
  21.8 0.0 collective-permute-done.near_ref
  21.8 1.2 %early.1 = (f32[8,64]{1,0:T(8,128)S(1)}, f32[8,64]{1,0:T(8,128)S(1)}) custom-call(bf16[64,16384]{1,0:T(8,128)(2,1)S(1)} %copy-done, f32[1,16384]{1,0:T(1,128)S(1)} %get-tuple-element.13.gain_ref, bf16[8,16384]{1,0:T(8,128)(2,1)S(1)} %collective-permute-done.near_ref, bf16[8,16384]{1,0:T(8,128)(2,1)S(1)} %collective-permute-done.1.far_ref), custom_call_target="tpu_custom_call" | custom-call | tf_op jit(solution)/shard_map/early/pallas_call | solution.py:80
  23.0 0.7 %collective-permute-done.2.cross = bf16[8,16384]{1,0:T(8,128)(2,1)S(1)} collective-permute-done((bf16[8,16384]{1,0:T(8,128)(2,1)S(1)}, bf16[8,16384]{1,0:T(8,128)(2,1)S(1)}, u32[]{:S(2)}, u32[]{:S(2)}) %collective-permute-start.2) | collective-permute-done | bytes 262176 | tf_op jit(solution)/shard_map/ppermute | solution.py:67
  23.7 1.3 %last.1 = (f32[16,32]{1,0:T(8,128)S(1)}, f32[16,32]{1,0:T(8,128)S(1)}, f32[16,32]{1,0:T(8,128)S(1)}, f32[16,32]{1,0:T(8,128)S(1)}) custom-call(s32[2]{0:T(128)S(1)} %pad_add_fusion.where_ref, s32[1]{0:T(128)S(6)} %copy.5.count_ref, bf16[64,16384]{1,0:T(8,128)(2,1)S(1)} %copy-done, f32[1,16384]{1,0:T(1,128)S(1)} %get-tuple-element.13.gain_ref, ...), custom_call_target="tpu_custom_call" | custom-call | tf_op jit(solution)/shard_map/last/pallas_call | solution.py:90
  25.0 0.1 collective-permute-start.3
  25.1 1.4 %collective-permute-start.4 = (f32[16,32]{1,0:T(8,128)S(1)}, f32[16,32]{1,0:T(8,128)S(1)}, u32[]{:S(2)}, u32[]{:S(2)}) collective-permute-start(f32[16,32]{1,0:T(8,128)S(1)} %get-tuple-element.19), channel_id=1, source_target_pairs={{0,8},{4,12},{8,0},{12,4},{1,9},{5,13},{9,1},{13,5},{2,10},{6,14},... | collective-permute-start | bytes 6152 | tf_op jit(solution)/shard_map/ppermute | solution.py:104
  26.4 0.5 %collective-permute-start.5 = (f32[16,32]{1,0:T(8,128)S(1)}, f32[16,32]{1,0:T(8,128)S(1)}, u32[]{:S(2)}, u32[]{:S(2)}) collective-permute-start(f32[16,32]{1,0:T(8,128)S(1)} %get-tuple-element.20), channel_id=1, source_target_pairs={{0,12},{4,8},{8,4},{12,0},{1,13},{5,9},{9,5},{13,1},{2,14},{6,10},... | collective-permute-start | bytes 6152 | tf_op jit(solution)/shard_map/ppermute | solution.py:104
  26.9 0.0 collective-permute-done.3
  26.9 1.9 %collective-permute-done.4 = f32[16,32]{1,0:T(8,128)S(1)} collective-permute-done((f32[16,32]{1,0:T(8,128)S(1)}, f32[16,32]{1,0:T(8,128)S(1)}, u32[]{:S(2)}, u32[]{:S(2)}) %collective-permute-start.4) | collective-permute-done | bytes 2080 | tf_op jit(solution)/shard_map/ppermute | solution.py:104
  28.8 0.7 %collective-permute-done.5 = f32[16,32]{1,0:T(8,128)S(1)} collective-permute-done((f32[16,32]{1,0:T(8,128)S(1)}, f32[16,32]{1,0:T(8,128)S(1)}, u32[]{:S(2)}, u32[]{:S(2)}) %collective-permute-start.5) | collective-permute-done | bytes 2080 | tf_op jit(solution)/shard_map/ppermute | solution.py:104
  29.5 0.6 %add_add_fusion = f32[16,32]{1,0:T(8,128)} fusion(f32[16,32]{1,0:T(8,128)S(1)} %collective-permute-done.5, f32[16,32]{1,0:T(8,128)S(1)} %collective-permute-done.4, f32[16,32]{1,0:T(8,128)S(1)} %get-tuple-element.17, f32[16,32]{1,0:T(8,128)S(1)} %collective-permute-done.3), kind=kLoop, calls=%fused_computation | loop fusion | flops 1536 | bytes 10240 | tf_op jit(solution)/shard_map/add | solution.py:104
Async XLA Ops:
  0.0 16.3 %collective-permute-start.1 = (bf16[8,16384]{1,0:T(8,128)(2,1)}, bf16[8,16384]{1,0:T(8,128)(2,1)S(1)}, u32[]{:S(2)}, u32[]{:S(2)}) collective-permute-start(bf16[8,16384]{1,0:T(8,128)(2,1)} %own_ref.1), channel_id=1, source_target_pairs={{0,2},{1,3},{2,0},{3,1},{4,6},{5,7},{6,4},{7,5},{8,10},{9,11},{10,... | collective-permute-start | bytes 786440 | tf_op jit(solution)/shard_map/ppermute | solution.py:67
  4.1 17.7 %collective-permute-start = (bf16[8,16384]{1,0:T(8,128)(2,1)}, bf16[8,16384]{1,0:T(8,128)(2,1)S(1)}, u32[]{:S(2)}, u32[]{:S(2)}) collective-permute-start(bf16[8,16384]{1,0:T(8,128)(2,1)} %own_ref.1), channel_id=1, source_target_pairs={{0,1},{1,0},{2,3},{3,2},{4,5},{5,4},{6,7},{7,6},{8,9},{9,8},{10,11... | collective-permute-start | bytes 786440 | tf_op jit(solution)/shard_map/ppermute | solution.py:67
  16.3 7.4 %collective-permute-start.2 = (bf16[8,16384]{1,0:T(8,128)(2,1)S(1)}, bf16[8,16384]{1,0:T(8,128)(2,1)S(1)}, u32[]{:S(2)}, u32[]{:S(2)}) collective-permute-start(bf16[8,16384]{1,0:T(8,128)(2,1)S(1)} %collective-permute-done.1.far_ref), channel_id=1, source_target_pairs={{0,1},{1,0},{2,3},{3,2},{4,5},{5,4},{6,7},{7,6},{8,9},{9,8},{10,11... | collective-permute-start | bytes 786440 | tf_op jit(solution)/shard_map/ppermute | solution.py:67
  17.7 1.6 %copy-start = (bf16[64,16384]{1,0:T(8,128)(2,1)S(1)}, bf16[64,16384]{1,0:T(8,128)(2,1)}, u32[]{:S(2)}) copy-start(bf16[64,16384]{1,0:T(8,128)(2,1)} %train_ref.5) | copy-start | bytes 6291460
  19.3 0.9 %copy-start.1 = (bf16[8,16384]{1,0:T(8,128)(2,1)S(1)}, bf16[8,16384]{1,0:T(8,128)(2,1)}, u32[]{:S(2)}) copy-start(bf16[8,16384]{1,0:T(8,128)(2,1)} %own_ref.1) | copy-start | bytes 786436
  20.2 0.8 %copy-start.2 = (f32[16384]{0:T(1024)S(1)}, f32[16384]{0:T(1024)}, u32[]{:S(2)}) copy-start(f32[16384]{0:T(1024)} %param.6) | copy-start | bytes 196612
  25.0 1.9 %collective-permute-start.3 = (f32[16,32]{1,0:T(8,128)S(1)}, f32[16,32]{1,0:T(8,128)S(1)}, u32[]{:S(2)}, u32[]{:S(2)}) collective-permute-start(f32[16,32]{1,0:T(8,128)S(1)} %get-tuple-element.18), channel_id=1, source_target_pairs={{0,4},{4,0},{8,12},{12,8},{1,5},{5,1},{9,13},{13,9},{2,6},{6,2},{1... | collective-permute-start | bytes 6152 | tf_op jit(solution)/shard_map/ppermute | solution.py:104
  25.1 3.7 %collective-permute-start.4 = (f32[16,32]{1,0:T(8,128)S(1)}, f32[16,32]{1,0:T(8,128)S(1)}, u32[]{:S(2)}, u32[]{:S(2)}) collective-permute-start(f32[16,32]{1,0:T(8,128)S(1)} %get-tuple-element.19), channel_id=1, source_target_pairs={{0,8},{4,12},{8,0},{12,4},{1,9},{5,13},{9,1},{13,5},{2,10},{6,14},... | collective-permute-start | bytes 6152 | tf_op jit(solution)/shard_map/ppermute | solution.py:104
  26.4 3.1 %collective-permute-start.5 = (f32[16,32]{1,0:T(8,128)S(1)}, f32[16,32]{1,0:T(8,128)S(1)}, u32[]{:S(2)}, u32[]{:S(2)}) collective-permute-start(f32[16,32]{1,0:T(8,128)S(1)} %get-tuple-element.20), channel_id=1, source_target_pairs={{0,12},{4,8},{8,4},{12,0},{1,13},{5,9},{9,5},{13,1},{2,14},{6,10},... | collective-permute-start | bytes 6152 | tf_op jit(solution)/shard_map/ppermute | solution.py:104

commit v3 on v2

v3 whole, which is shorter than its diff:
```python
import functools

import jax
import jax.numpy as jnp
from jax import lax
from jax.experimental import pallas as pl
from jax.experimental.pallas import tpu as pltpu
from jax.sharding import PartitionSpec as P

damping_term = 0.1
vmem = pl.BlockSpec(memory_space=pltpu.VMEM)
smem = pl.BlockSpec(memory_space=pltpu.SMEM)
grant = pltpu.CompilerParams(vmem_limit_bytes=16 << 20)


def product(rows, piece):
    return lax.dot_general(
        rows, piece, (((1,), (1,)), ((), ())), preferred_element_type=jnp.float32
    )


def gathered(train_grads, query_grads, curvature, row_counts):
    slots = train_grads.shape[0]
    live = (jnp.arange(slots, dtype=jnp.int32) < row_counts[0])[:, None]
    queries = lax.all_gather(query_grads, "loop", axis=0, tiled=True).astype(jnp.float32)
    scaled = (queries / (damping_term + curvature[None, :])).astype(jnp.bfloat16)
    partial_scores = jnp.where(live, product(train_grads, scaled), jnp.float32(0.0))
    return lax.psum_scatter(partial_scores, "feat", scatter_dimension=0, tiled=True)


def scored(piece_ref, gain_ref, train_ref, start=0):
    span = pl.ds(start, piece_ref.shape[1])
    scaled = (piece_ref[...].astype(jnp.float32) * gain_ref[:, span]).astype(jnp.bfloat16)
    return product(scaled, train_ref[:, span])


def own_kernel(train_ref, curve_ref, own_ref, score_ref, gain_ref):
    gain_ref[...] = 1.0 / (damping_term + curve_ref[...])
    score_ref[...] = scored(own_ref, gain_ref, train_ref)


def early_kernel(train_ref, gain_ref, near, *refs):
    fars, near_score, far_score = refs[:-2], refs[-2], refs[-1]
    near_score[...] = scored(near, gain_ref, train_ref)
    start, total = 0, 0.0
    for far in fars:
        total = total + scored(far, gain_ref, train_ref, start)
        start += far.shape[1]
    far_score[...] = total


def mid_kernel(train_ref, gain_ref, *refs):
    start, total = 0, 0.0
    for cross in refs[:-1]:
        total = total + scored(cross, gain_ref, train_ref, start)
        start += cross.shape[1]
    refs[-1][...] = total


def last_kernel(count_ref, train_ref, gain_ref, own, near, far, cross, final, *refs):
    outs, table, scores = refs[:-2], refs[-2], refs[-1]
    me, part = lax.axis_index("loop"), lax.axis_index("feat")
    slots, features = train_ref.shape
    table[me] = own[...]
    table[me ^ 1] = near[...]
    table[me ^ 2] = far[...]
    table[me ^ 3] = cross[...] + scored(final, gain_ref, train_ref, features - final.shape[1])
    whole = table[...].reshape(-1, slots).T
    live = lax.broadcasted_iota(jnp.int32, whole.shape, 0) < count_ref[0]
    scores[...] = jnp.where(live, whole, 0.0)
    height = outs[0].shape[0]
    for hop, out in enumerate(outs):
        out[...] = scores[pl.ds(pl.multiple_of((part ^ hop) * height, height), height), :]


shares = (3, 3, 2)


def permuted(n_feat, train_grads, query_grads, curvature, row_counts):
    slots, features = train_grads.shape
    rows = query_grads.shape[0]

    def swap(piece, axis, mask):
        pairs = [(i, i ^ mask) for i in range(lax.axis_size(axis))]
        return lax.ppermute(piece, axis, pairs)

    def kernel(body, shapes, operands, smems=0, scratch=()):
        return pl.pallas_call(
            body,
            out_shape=shapes,
            in_specs=[smem] * smems + [vmem] * (len(operands) - smems),
            out_specs=[vmem] * len(shapes),
            scratch_shapes=scratch,
            compiler_params=grant,
        )(*operands)

    score = jax.ShapeDtypeStruct((rows, slots), jnp.float32)
    near = swap(query_grads, "loop", 1)
    ends = [features * sum(shares[: k + 1]) // sum(shares) for k in range(len(shares))]
    chunks, after = [], query_grads
    for start, end in zip([0] + ends, ends):
        chunks.append(after[:, start:end])
        after, _ = lax.optimization_barrier((after, chunks[-1]))
    far = [swap(chunk, "loop", 2) for chunk in chunks]
    own_score, gain = kernel(
        own_kernel,
        [score, jax.ShapeDtypeStruct((1, features), jnp.float32)],
        (train_grads, curvature[None, :], query_grads),
    )
    cross = [swap(piece, "loop", 1) for piece in far]
    near_score, far_score = kernel(early_kernel, [score] * 2, (train_grads, gain, near, *far))
    (cross_score,) = kernel(mid_kernel, [score], (train_grads, gain, *cross[:-1]))
    block = jax.ShapeDtypeStruct((slots // n_feat, 4 * rows), jnp.float32)
    blocks = kernel(
        last_kernel,
        [block] * n_feat,
        (row_counts, train_grads, gain, own_score, near_score, far_score, cross_score, cross[-1]),
        smems=1,
        scratch=[
            pltpu.VMEM((4, rows, slots), jnp.float32),
            pltpu.VMEM((slots, 4 * rows), jnp.float32),
        ],
    )
    total = blocks[0]
    for hop in range(1, n_feat):
        total = total + swap(blocks[hop], "feat", hop)
    return total


def solution(mesh):
    placed = (
        P(("groups", "loop"), "feat"),
        P(("groups", "loop"), "feat"),
        P("feat"),
        P(("groups", "loop")),
    )
    n_loop, n_feat = mesh.shape["loop"], mesh.shape["feat"]
    short = n_loop == 4 and n_feat & (n_feat - 1) == 0
    return jax.shard_map(
        functools.partial(permuted, n_feat) if short else gathered,
        mesh=mesh,
        in_specs=placed,
        out_specs=P(("groups", "loop", "feat"), None),
        check_vma=False,
    )
```

time: 30.3 us -> 33.4 us (1.10)
  starting transfers between devices: 8.29 us -> 15.6 us
  waiting for transfers between devices: 14 us -> 7.42 us
  local copies, waits for them, and re-layouts: 3.37 us -> 6.05 us
  Pallas kernels: 3.12 us -> 2.74 us
    ppermute x6 -> x10, starting transfers between devices: 8.29 us -> 15.6 us  [swap(): return lax.ppermute(piece, axis, pairs)]
    ppermute x6 -> x10, waiting for transfers between devices: 14 us -> 7.42 us  [swap(): return lax.ppermute(piece, axis, pairs)]
    slice x0 -> x3, local copies, waits for them, and re-layouts: none -> 2.68 us  [permuted(): chunks.append(after[:, start:end])]
    pallas_call x3 -> x4, Pallas kernels: 3.12 us -> 2.74 us  [kernel(): pl.pallas_call(body, out_shape=shapes, in_specs=[smem] * smems + [vmem] *...]
  transfers between devices with their start and end apart: 6 -> 10, of which waited for: 4 -> 5; matrix products, arithmetic and copies ran while one was open for 0% -> 8% of each run, Pallas kernels for 6% -> 7%
where the time goes in v3:
time: 33.4 us; the launch traced here: 33.1 us
  starting transfers between devices  15.6 us (47%)
  waiting for transfers between devices  7.42 us (22%)
  local copies, waits for them, and re-layouts  6.05 us (18%)
  Pallas kernels  2.74 us (8%)
  between operations  0.7 us (2%)
  other arithmetic  0.6 us (2%)
    ppermute x10, starting transfers between devices, swap(): return lax.ppermute(piece, axis, pairs)  15.6 us
    ppermute x10, waiting for transfers between devices, swap(): return lax.ppermute(piece, axis, pairs)  7.42 us
    unnamed x6, local copies, waits for them, and re-layouts  3.37 us
    pallas_call x4, Pallas kernels, kernel(): pl.pallas_call(body, out_shape=shapes, in_specs=[smem] * smems + [vmem] *...  2.74 us
    slice x3, local copies, waits for them, and re-layouts, permuted(): chunks.append(after[:, start:end])  2.68 us
  transfers between devices with their start and end apart: 10, of which 5 were waited for; matrix products, arithmetic and copies ran while one was open for 8% of the time, Pallas kernels for 7%

profile of v3, /device:TPU:0, one launch (start us, length us, event | category | flops | bytes accessed | tf_op | source)
XLA Modules:
  0.0 33.1 jit_solution(2343678578395000431)
XLA Ops:
  0.0 3.1 %collective-permute-start = (bf16[8,16384]{1,0:T(8,128)(2,1)}, bf16[8,16384]{1,0:T(8,128)(2,1)S(1)}, u32[]{:S(2)}, u32[]{:S(2)}) collective-permute-start(bf16[8,16384]{1,0:T(8,128)(2,1)} %own_ref.1), channel_id=1, source_target_pairs={{0,1},{1,0},{2,3},{3,2},{4,5},{5,4},{6,7},{7,6},{8,9},{9,8},{10,11... | collective-permute-start | bytes 786440 | tf_op jit(solution)/shard_map/ppermute | solution.py:85
  3.1 0.9 %slice.9 = bf16[8,6144]{1,0:T(8,128)(2,1)S(1)} slice(bf16[8,16384]{1,0:T(8,128)(2,1)} %own_ref.1), slice={[0:8], [0:6144]} | slice | bytes 196608 | tf_op jit(solution)/shard_map/slice | solution.py:102
  4.0 0.9 %slice.10 = bf16[8,6144]{1,0:T(8,128)(2,1)S(1)} slice(bf16[8,16384]{1,0:T(8,128)(2,1)} %own_ref.1), slice={[0:8], [6144:12288]} | slice | bytes 196608 | tf_op jit(solution)/shard_map/slice | solution.py:102
  4.9 2.6 %collective-permute-start.2 = (bf16[8,6144]{1,0:T(8,128)(2,1)S(1)}, bf16[8,6144]{1,0:T(8,128)(2,1)S(1)}, u32[]{:S(2)}, u32[]{:S(2)}) collective-permute-start(bf16[8,6144]{1,0:T(8,128)(2,1)S(1)} %slice.10), channel_id=1, source_target_pairs={{0,2},{1,3},{2,0},{3,1},{4,6},{5,7},{6,4},{7,5},{8,10},{9,11},{10,... | collective-permute-start | bytes 294920 | tf_op jit(solution)/shard_map/ppermute | solution.py:85
  7.5 0.3 %collective-permute-start.1 = (bf16[8,6144]{1,0:T(8,128)(2,1)S(1)}, bf16[8,6144]{1,0:T(8,128)(2,1)S(1)}, u32[]{:S(2)}, u32[]{:S(2)}) collective-permute-start(bf16[8,6144]{1,0:T(8,128)(2,1)S(1)} %slice.9), channel_id=1, source_target_pairs={{0,2},{1,3},{2,0},{3,1},{4,6},{5,7},{6,4},{7,5},{8,10},{9,11},{10,... | collective-permute-start | bytes 294920 | tf_op jit(solution)/shard_map/ppermute | solution.py:85
  7.8 0.8 %slice.11 = bf16[8,4096]{1,0:T(8,128)(2,1)S(1)} slice(bf16[8,16384]{1,0:T(8,128)(2,1)} %own_ref.1), slice={[0:8], [12288:16384]} | slice | bytes 131072 | tf_op jit(solution)/shard_map/slice | solution.py:102
  8.7 2.6 %collective-permute-start.3 = (bf16[8,4096]{1,0:T(8,128)(2,1)S(1)}, bf16[8,4096]{1,0:T(8,128)(2,1)S(1)}, u32[]{:S(2)}, u32[]{:S(2)}) collective-permute-start(bf16[8,4096]{1,0:T(8,128)(2,1)S(1)} %slice.11), channel_id=1, source_target_pairs={{0,2},{1,3},{2,0},{3,1},{4,6},{5,7},{6,4},{7,5},{8,10},{9,11},{10,... | collective-permute-start | bytes 196616 | tf_op jit(solution)/shard_map/ppermute | solution.py:85
  11.2 0.9 %collective-permute-done.2.refs_1_ = bf16[8,6144]{1,0:T(8,128)(2,1)S(1)} collective-permute-done((bf16[8,6144]{1,0:T(8,128)(2,1)S(1)}, bf16[8,6144]{1,0:T(8,128)(2,1)S(1)}, u32[]{:S(2)}, u32[]{:S(2)}) %collective-permute-start.2) | collective-permute-done | bytes 98336 | tf_op jit(solution)/shard_map/ppermute | solution.py:85
  12.1 3.8 %collective-permute-start.5 = (bf16[8,6144]{1,0:T(8,128)(2,1)S(1)}, bf16[8,6144]{1,0:T(8,128)(2,1)S(1)}, u32[]{:S(2)}, u32[]{:S(2)}) collective-permute-start(bf16[8,6144]{1,0:T(8,128)(2,1)S(1)} %collective-permute-done.2.refs_1_), channel_id=1, source_target_pairs={{0,1},{1,0},{2,3},{3,2},{4,5},{5,4},{6,7},{7,6},{8,9},{9,8},{10,11... | collective-permute-start | bytes 294920 | tf_op jit(solution)/shard_map/ppermute | solution.py:85
  15.9 3.1 %collective-permute-done.1.refs_0_ = bf16[8,6144]{1,0:T(8,128)(2,1)S(1)} collective-permute-done((bf16[8,6144]{1,0:T(8,128)(2,1)S(1)}, bf16[8,6144]{1,0:T(8,128)(2,1)S(1)}, u32[]{:S(2)}, u32[]{:S(2)}) %collective-permute-start.1) | collective-permute-done | bytes 98336 | tf_op jit(solution)/shard_map/ppermute | solution.py:85
  18.9 0.0 collective-permute-start.4
  18.9 0.7 %collective-permute-done.3.refs_2_ = bf16[8,4096]{1,0:T(8,128)(2,1)S(1)} collective-permute-done((bf16[8,4096]{1,0:T(8,128)(2,1)S(1)}, bf16[8,4096]{1,0:T(8,128)(2,1)S(1)}, u32[]{:S(2)}, u32[]{:S(2)}) %collective-permute-start.3) | collective-permute-done | bytes 65568 | tf_op jit(solution)/shard_map/ppermute | solution.py:85
  19.6 1.3 %collective-permute-start.6 = (bf16[8,4096]{1,0:T(8,128)(2,1)S(1)}, bf16[8,4096]{1,0:T(8,128)(2,1)S(1)}, u32[]{:S(2)}, u32[]{:S(2)}) collective-permute-start(bf16[8,4096]{1,0:T(8,128)(2,1)S(1)} %collective-permute-done.3.refs_2_), channel_id=1, source_target_pairs={{0,1},{1,0},{2,3},{3,2},{4,5},{5,4},{6,7},{7,6},{8,9},{9,8},{10,11... | collective-permute-start | bytes 196616 | tf_op jit(solution)/shard_map/ppermute | solution.py:85
  21.6 0.0 copy-start
  21.6 1.6 %copy-done = bf16[64,16384]{1,0:T(8,128)(2,1)S(1)} copy-done((bf16[64,16384]{1,0:T(8,128)(2,1)S(1)}, bf16[64,16384]{1,0:T(8,128)(2,1)}, u32[]{:S(2)}) %copy-start) | copy-done | bytes 2097176
  23.2 0.9 %copy-done.1 = bf16[8,16384]{1,0:T(8,128)(2,1)S(1)} copy-done((bf16[8,16384]{1,0:T(8,128)(2,1)S(1)}, bf16[8,16384]{1,0:T(8,128)(2,1)}, u32[]{:S(2)}) %copy-start.1) | copy-done | bytes 262168
  24.2 0.8 %copy-done.2 = f32[16384]{0:T(1024)S(1)} copy-done((f32[16384]{0:T(1024)S(1)}, f32[16384]{0:T(1024)}, u32[]{:S(2)}) %copy-start.2) | copy-done | bytes 65560
  25.0 0.6 %shard_map.46 = (f32[8,64]{1,0:T(8,128)S(1)}, f32[1,16384]{1,0:T(1,128)S(1)}) custom-call(bf16[64,16384]{1,0:T(8,128)(2,1)S(1)} %copy-done, f32[1,16384]{1,0:T(1,128)S(1)} %bitcast.1, bf16[8,16384]{1,0:T(8,128)(2,1)S(1)} %copy-done.1), custom_call_target="tpu_custom_call" | custom-call | tf_op jit(solution)/shard_map/pallas_call | solution.py:88
  25.6 0.0 collective-permute-done.5.refs_1_
  25.6 0.0 collective-permute-done.4.refs_0_
  25.7 0.5 %shard_map.48.cross = f32[8,64]{1,0:T(8,128)S(1)} custom-call(bf16[64,16384]{1,0:T(8,128)(2,1)S(1)} %copy-done, f32[1,16384]{1,0:T(1,128)S(1)} %get-tuple-element.15.gain_ref, bf16[8,6144]{1,0:T(8,128)(2,1)S(1)} %collective-permute-done.4.refs_0_, bf16[8,6144]{1,0:T(8,128)(2,1)S(1)} %collective-permute-done.5.refs_1_), custom_call_target="tpu_custom_call" | custom-call | tf_op jit(solution)/shard_map/pallas_call | solution.py:88
  26.2 0.0 collective-permute-done.near
  26.2 1.2 %shard_map.47 = (f32[8,64]{1,0:T(8,128)S(1)}, f32[8,64]{1,0:T(8,128)S(1)}) custom-call(bf16[64,16384]{1,0:T(8,128)(2,1)S(1)} %copy-done, f32[1,16384]{1,0:T(1,128)S(1)} %get-tuple-element.15.gain_ref, bf16[8,16384]{1,0:T(8,128)(2,1)S(1)} %collective-permute-done.near, bf16[8,6144]{1,0:T(8,128)(2,1)S(1)} %collective-permute-done.1.refs_0_, ...), custom_call_target="tpu_custom_call" | custom-call | tf_op jit(solution)/shard_map/pallas_call | solution.py:88
  27.4 0.0 collective-permute-done.6.final
  27.4 0.4 %shard_map.49 = (f32[16,32]{1,0:T(8,128)S(1)}, f32[16,32]{1,0:T(8,128)S(1)}, f32[16,32]{1,0:T(8,128)S(1)}, f32[16,32]{1,0:T(8,128)S(1)}) custom-call(s32[1]{0:T(128)S(6)} %copy.5.count_ref, bf16[64,16384]{1,0:T(8,128)(2,1)S(1)} %copy-done, f32[1,16384]{1,0:T(1,128)S(1)} %get-tuple-element.15.gain_ref, f32[8,64]{1,0:T(8,128)S(1)} %get-tuple-element.16.own, ...), custom_call_target="tpu_custom_call" | custom-call | tf_op jit(solution)/shard_map/pallas_call | solution.py:88
  27.8 0.1 collective-permute-start.7
  27.8 1.6 %collective-permute-start.8 = (f32[16,32]{1,0:T(8,128)S(1)}, f32[16,32]{1,0:T(8,128)S(1)}, u32[]{:S(2)}, u32[]{:S(2)}) collective-permute-start(f32[16,32]{1,0:T(8,128)S(1)} %get-tuple-element.23), channel_id=1, source_target_pairs={{0,8},{4,12},{8,0},{12,4},{1,9},{5,13},{9,1},{13,5},{2,10},{6,14},... | collective-permute-start | bytes 6152 | tf_op jit(solution)/shard_map/ppermute | solution.py:85
  29.4 0.3 collective-permute-start.9
  29.7 0.0 collective-permute-done.7
  29.7 1.9 %collective-permute-done.8 = f32[16,32]{1,0:T(8,128)S(1)} collective-permute-done((f32[16,32]{1,0:T(8,128)S(1)}, f32[16,32]{1,0:T(8,128)S(1)}, u32[]{:S(2)}, u32[]{:S(2)}) %collective-permute-start.8) | collective-permute-done | bytes 2080 | tf_op jit(solution)/shard_map/ppermute | solution.py:85
  31.6 0.9 %collective-permute-done.9 = f32[16,32]{1,0:T(8,128)S(1)} collective-permute-done((f32[16,32]{1,0:T(8,128)S(1)}, f32[16,32]{1,0:T(8,128)S(1)}, u32[]{:S(2)}, u32[]{:S(2)}) %collective-permute-start.9) | collective-permute-done | bytes 2080 | tf_op jit(solution)/shard_map/ppermute | solution.py:85
  32.5 0.6 %add_add_fusion = f32[16,32]{1,0:T(8,128)} fusion(f32[16,32]{1,0:T(8,128)S(1)} %collective-permute-done.9, f32[16,32]{1,0:T(8,128)S(1)} %collective-permute-done.8, f32[16,32]{1,0:T(8,128)S(1)} %get-tuple-element.21, f32[16,32]{1,0:T(8,128)S(1)} %collective-permute-done.7), kind=kLoop, calls=%fused_computation | loop fusion | flops 1536 | bytes 10240 | tf_op jit(solution)/shard_map/add | solution.py:126
  (2 shorter events, 0.0 us)
Async XLA Ops:
  0.0 26.2 %collective-permute-start = (bf16[8,16384]{1,0:T(8,128)(2,1)}, bf16[8,16384]{1,0:T(8,128)(2,1)S(1)}, u32[]{:S(2)}, u32[]{:S(2)}) collective-permute-start(bf16[8,16384]{1,0:T(8,128)(2,1)} %own_ref.1), channel_id=1, source_target_pairs={{0,1},{1,0},{2,3},{3,2},{4,5},{5,4},{6,7},{7,6},{8,9},{9,8},{10,11... | collective-permute-start | bytes 786440 | tf_op jit(solution)/shard_map/ppermute | solution.py:85
  4.9 7.2 %collective-permute-start.2 = (bf16[8,6144]{1,0:T(8,128)(2,1)S(1)}, bf16[8,6144]{1,0:T(8,128)(2,1)S(1)}, u32[]{:S(2)}, u32[]{:S(2)}) collective-permute-start(bf16[8,6144]{1,0:T(8,128)(2,1)S(1)} %slice.10), channel_id=1, source_target_pairs={{0,2},{1,3},{2,0},{3,1},{4,6},{5,7},{6,4},{7,5},{8,10},{9,11},{10,... | collective-permute-start | bytes 294920 | tf_op jit(solution)/shard_map/ppermute | solution.py:85
  7.5 11.5 %collective-permute-start.1 = (bf16[8,6144]{1,0:T(8,128)(2,1)S(1)}, bf16[8,6144]{1,0:T(8,128)(2,1)S(1)}, u32[]{:S(2)}, u32[]{:S(2)}) collective-permute-start(bf16[8,6144]{1,0:T(8,128)(2,1)S(1)} %slice.9), channel_id=1, source_target_pairs={{0,2},{1,3},{2,0},{3,1},{4,6},{5,7},{6,4},{7,5},{8,10},{9,11},{10,... | collective-permute-start | bytes 294920 | tf_op jit(solution)/shard_map/ppermute | solution.py:85
  8.7 11.0 %collective-permute-start.3 = (bf16[8,4096]{1,0:T(8,128)(2,1)S(1)}, bf16[8,4096]{1,0:T(8,128)(2,1)S(1)}, u32[]{:S(2)}, u32[]{:S(2)}) collective-permute-start(bf16[8,4096]{1,0:T(8,128)(2,1)S(1)} %slice.11), channel_id=1, source_target_pairs={{0,2},{1,3},{2,0},{3,1},{4,6},{5,7},{6,4},{7,5},{8,10},{9,11},{10,... | collective-permute-start | bytes 196616 | tf_op jit(solution)/shard_map/ppermute | solution.py:85
  12.1 13.5 %collective-permute-start.5 = (bf16[8,6144]{1,0:T(8,128)(2,1)S(1)}, bf16[8,6144]{1,0:T(8,128)(2,1)S(1)}, u32[]{:S(2)}, u32[]{:S(2)}) collective-permute-start(bf16[8,6144]{1,0:T(8,128)(2,1)S(1)} %collective-permute-done.2.refs_1_), channel_id=1, source_target_pairs={{0,1},{1,0},{2,3},{3,2},{4,5},{5,4},{6,7},{7,6},{8,9},{9,8},{10,11... | collective-permute-start | bytes 294920 | tf_op jit(solution)/shard_map/ppermute | solution.py:85
  18.9 6.7 %collective-permute-start.4 = (bf16[8,6144]{1,0:T(8,128)(2,1)S(1)}, bf16[8,6144]{1,0:T(8,128)(2,1)S(1)}, u32[]{:S(2)}, u32[]{:S(2)}) collective-permute-start(bf16[8,6144]{1,0:T(8,128)(2,1)S(1)} %collective-permute-done.1.refs_0_), channel_id=1, source_target_pairs={{0,1},{1,0},{2,3},{3,2},{4,5},{5,4},{6,7},{7,6},{8,9},{9,8},{10,11... | collective-permute-start | bytes 294920 | tf_op jit(solution)/shard_map/ppermute | solution.py:85
  19.6 7.8 %collective-permute-start.6 = (bf16[8,4096]{1,0:T(8,128)(2,1)S(1)}, bf16[8,4096]{1,0:T(8,128)(2,1)S(1)}, u32[]{:S(2)}, u32[]{:S(2)}) collective-permute-start(bf16[8,4096]{1,0:T(8,128)(2,1)S(1)} %collective-permute-done.3.refs_2_), channel_id=1, source_target_pairs={{0,1},{1,0},{2,3},{3,2},{4,5},{5,4},{6,7},{7,6},{8,9},{9,8},{10,11... | collective-permute-start | bytes 196616 | tf_op jit(solution)/shard_map/ppermute | solution.py:85
  21.6 1.6 %copy-start = (bf16[64,16384]{1,0:T(8,128)(2,1)S(1)}, bf16[64,16384]{1,0:T(8,128)(2,1)}, u32[]{:S(2)}) copy-start(bf16[64,16384]{1,0:T(8,128)(2,1)} %train_ref.7) | copy-start | bytes 6291460
  23.2 0.9 %copy-start.1 = (bf16[8,16384]{1,0:T(8,128)(2,1)S(1)}, bf16[8,16384]{1,0:T(8,128)(2,1)}, u32[]{:S(2)}) copy-start(bf16[8,16384]{1,0:T(8,128)(2,1)} %own_ref.1) | copy-start | bytes 786436
  24.2 0.8 %copy-start.2 = (f32[16384]{0:T(1024)S(1)}, f32[16384]{0:T(1024)}, u32[]{:S(2)}) copy-start(f32[16384]{0:T(1024)} %param.6) | copy-start | bytes 196612
  27.8 1.9 %collective-permute-start.7 = (f32[16,32]{1,0:T(8,128)S(1)}, f32[16,32]{1,0:T(8,128)S(1)}, u32[]{:S(2)}, u32[]{:S(2)}) collective-permute-start(f32[16,32]{1,0:T(8,128)S(1)} %get-tuple-element.22), channel_id=1, source_target_pairs={{0,4},{4,0},{8,12},{12,8},{1,5},{5,1},{9,13},{13,9},{2,6},{6,2},{1... | collective-permute-start | bytes 6152 | tf_op jit(solution)/shard_map/ppermute | solution.py:85
  27.8 3.7 %collective-permute-start.8 = (f32[16,32]{1,0:T(8,128)S(1)}, f32[16,32]{1,0:T(8,128)S(1)}, u32[]{:S(2)}, u32[]{:S(2)}) collective-permute-start(f32[16,32]{1,0:T(8,128)S(1)} %get-tuple-element.23), channel_id=1, source_target_pairs={{0,8},{4,12},{8,0},{12,4},{1,9},{5,13},{9,1},{13,5},{2,10},{6,14},... | collective-permute-start | bytes 6152 | tf_op jit(solution)/shard_map/ppermute | solution.py:85
  29.4 3.1 %collective-permute-start.9 = (f32[16,32]{1,0:T(8,128)S(1)}, f32[16,32]{1,0:T(8,128)S(1)}, u32[]{:S(2)}, u32[]{:S(2)}) collective-permute-start(f32[16,32]{1,0:T(8,128)S(1)} %get-tuple-element.24), channel_id=1, source_target_pairs={{0,12},{4,8},{8,4},{12,0},{1,13},{5,9},{9,5},{13,1},{2,14},{6,10},... | collective-permute-start | bytes 6152 | tf_op jit(solution)/shard_map/ppermute | solution.py:85

commit v4 on v3

--- a/solution.py
+++ b/solution.py
@@ -34,19 +34,25 @@
     return product(scaled, train_ref[:, span])
 
 
-def own_kernel(train_ref, curve_ref, own_ref, score_ref, gain_ref):
+def own_kernel(train_ref, curve_ref, *refs):
+    pieces, score_ref, gain_ref = refs[:-2], refs[-2], refs[-1]
     gain_ref[...] = 1.0 / (damping_term + curve_ref[...])
-    score_ref[...] = scored(own_ref, gain_ref, train_ref)
+    start, total = 0, 0.0
+    for piece in pieces:
+        total = total + scored(piece, gain_ref, train_ref, start)
+        start += piece.shape[1]
+    score_ref[...] = total
 
 
-def early_kernel(train_ref, gain_ref, near, *refs):
-    fars, near_score, far_score = refs[:-2], refs[-2], refs[-1]
-    near_score[...] = scored(near, gain_ref, train_ref)
-    start, total = 0, 0.0
-    for far in fars:
-        total = total + scored(far, gain_ref, train_ref, start)
-        start += far.shape[1]
-    far_score[...] = total
+def early_kernel(train_ref, gain_ref, *refs):
+    pieces, sums = refs[:-2], refs[-2:]
+    half = len(pieces) // 2
+    for group, out in zip((pieces[:half], pieces[half:]), sums):
+        start, total = 0, 0.0
+        for piece in group:
+            total = total + scored(piece, gain_ref, train_ref, start)
+            start += piece.shape[1]
+        out[...] = total
 
 
 def mid_kernel(train_ref, gain_ref, *refs):
@@ -73,7 +79,7 @@
         out[...] = scores[pl.ds(pl.multiple_of((part ^ hop) * height, height), height), :]
 
 
-shares = (3, 3, 2)
+shares = (1, 1)
 
 
 def permuted(n_feat, train_grads, query_grads, curvature, row_counts):
@@ -95,20 +101,35 @@
         )(*operands)
 
     score = jax.ShapeDtypeStruct((rows, slots), jnp.float32)
-    near = swap(query_grads, "loop", 1)
     ends = [features * sum(shares[: k + 1]) // sum(shares) for k in range(len(shares))]
     chunks, after = [], query_grads
     for start, end in zip([0] + ends, ends):
         chunks.append(after[:, start:end])
         after, _ = lax.optimization_barrier((after, chunks[-1]))
-    far = [swap(chunk, "loop", 2) for chunk in chunks]
+    n_loop = lax.axis_size("loop")
+
+    def turns(piece, even, odd):
+        pairs = [
+            (part * n_loop + i, part * n_loop + (i ^ (odd if part & 1 else even)))
+            for part in range(n_feat)
+            for i in range(n_loop)
+        ]
+        return lax.ppermute(piece, ("feat", "loop"), pairs)
+
+    odd = lax.axis_index("feat") & 1 == 1
+    first = turns(chunks[0], 1, 2)
+    second = turns(chunks[0], 2, 1)
+    pick = lambda on_odd, on_even: jnp.where(odd, on_odd, on_even)
+    far0, near0 = pick(first, second), pick(second, first)
+    far = [far0] + [swap(chunk, "loop", 2) for k, chunk in enumerate(chunks) if k]
+    near = [near0] + [swap(chunk, "loop", 1) for k, chunk in enumerate(chunks) if k]
     own_score, gain = kernel(
         own_kernel,
         [score, jax.ShapeDtypeStruct((1, features), jnp.float32)],
-        (train_grads, curvature[None, :], query_grads),
+        (train_grads, curvature[None, :], *chunks),
     )
     cross = [swap(piece, "loop", 1) for piece in far]
-    near_score, far_score = kernel(early_kernel, [score] * 2, (train_grads, gain, near, *far))
+    near_score, far_score = kernel(early_kernel, [score] * 2, (train_grads, gain, *near, *far))
     (cross_score,) = kernel(mid_kernel, [score], (train_grads, gain, *cross[:-1]))
     block = jax.ShapeDtypeStruct((slots // n_feat, 4 * rows), jnp.float32)
     blocks = kernel(

time: 33.4 us -> 29.8 us (0.89)
  starting transfers between devices: 15.6 us -> 12.9 us
  local copies, waits for them, and re-layouts: 6.05 us -> 4.25 us
  waiting for transfers between devices: 7.42 us -> 8.4 us
    ppermute x10 -> x7, starting transfers between devices: 15.6 us -> 7.18 us  [swap(): return lax.ppermute(piece, axis, pairs)]
    ppermute x0 -> x2, starting transfers between devices: none -> 5.71 us  [turns(): return lax.ppermute(piece, ('feat', 'loop'), pairs)]
    ppermute x0 -> x2, waiting for transfers between devices: none -> 3.74 us  [turns(): return lax.ppermute(piece, ('feat', 'loop'), pairs)]
    ppermute x10 -> x7, waiting for transfers between devices: 7.42 us -> 4.66 us  [swap(): return lax.ppermute(piece, axis, pairs)]
    unnamed x6 -> x4, local copies, waits for them, and re-layouts: 3.37 us -> 2.43 us
    slice x3 -> x2, local copies, waits for them, and re-layouts: 2.68 us -> 1.83 us  [permuted(): chunks.append(after[:, start:end])]
  transfers between devices with their start and end apart: 10 -> 9, of which waited for: 5 -> 5; matrix products, arithmetic and copies ran while one was open for 8% -> 3% of each run, Pallas kernels for 7% -> 8%
where the time goes in v4:
time: 29.8 us; the launch traced here: 29.6 us
  starting transfers between devices  12.9 us (43%)
  waiting for transfers between devices  8.4 us (28%)
  local copies, waits for them, and re-layouts  4.25 us (14%)
  Pallas kernels  2.72 us (9%)
  between operations  0.7 us (2%)
  other arithmetic  0.63 us (2%)
    ppermute x7, starting transfers between devices, swap(): return lax.ppermute(piece, axis, pairs)  7.18 us
    ppermute x2, starting transfers between devices, turns(): return lax.ppermute(piece, ('feat', 'loop'), pairs)  5.71 us
    ppermute x7, waiting for transfers between devices, swap(): return lax.ppermute(piece, axis, pairs)  4.66 us
    ppermute x2, waiting for transfers between devices, turns(): return lax.ppermute(piece, ('feat', 'loop'), pairs)  3.74 us
    pallas_call x4, Pallas kernels, kernel(): pl.pallas_call(body, out_shape=shapes, in_specs=[smem] * smems + [vmem] *...  2.72 us
    unnamed x4, local copies, waits for them, and re-layouts  2.43 us
    slice x2, local copies, waits for them, and re-layouts, permuted(): chunks.append(after[:, start:end])  1.83 us
    add x1, other arithmetic, permuted(): total = total + swap(blocks[hop], 'feat', hop)  0.6 us
  transfers between devices with their start and end apart: 9, of which 5 were waited for; matrix products, arithmetic and copies ran while one was open for 3% of the time, Pallas kernels for 8%

profile of v4, /device:TPU:0, one launch (start us, length us, event | category | flops | bytes accessed | tf_op | source)
XLA Modules:
  0.0 29.6 jit_solution(865704756021246763)
XLA Ops:
  0.0 0.9 %slice.6.refs_0_ = bf16[8,8192]{1,0:T(8,128)(2,1)S(1)} slice(bf16[8,16384]{1,0:T(8,128)(2,1)} %param.5), slice={[0:8], [0:8192]} | slice | bytes 262144 | tf_op jit(solution)/shard_map/slice | solution.py:107
  0.9 4.1 %collective-permute-start = (bf16[8,8192]{1,0:T(8,128)(2,1)S(1)}, bf16[8,8192]{1,0:T(8,128)(2,1)S(1)}, u32[]{:S(2)}, u32[]{:S(2)}) collective-permute-start(bf16[8,8192]{1,0:T(8,128)(2,1)S(1)} %slice.6.refs_0_), channel_id=1, source_target_pairs={{0,2},{1,3},{2,0},{3,1},{4,5},{5,4},{6,7},{7,6},{8,10},{9,11},{10,... | collective-permute-start | bytes 393224 | tf_op jit(solution)/shard_map/ppermute | solution.py:117
  5.0 1.6 %collective-permute-start.1 = (bf16[8,8192]{1,0:T(8,128)(2,1)S(1)}, bf16[8,8192]{1,0:T(8,128)(2,1)S(1)}, u32[]{:S(2)}, u32[]{:S(2)}) collective-permute-start(bf16[8,8192]{1,0:T(8,128)(2,1)S(1)} %slice.6.refs_0_), channel_id=1, source_target_pairs={{0,1},{1,0},{2,3},{3,2},{4,6},{5,7},{6,4},{7,5},{8,9},{9,8},{10,11... | collective-permute-start | bytes 393224 | tf_op jit(solution)/shard_map/ppermute | solution.py:117
  6.6 0.9 %slice.7.refs_1_ = bf16[8,8192]{1,0:T(8,128)(2,1)S(1)} slice(bf16[8,16384]{1,0:T(8,128)(2,1)} %param.5), slice={[0:8], [8192:16384]} | slice | bytes 262144 | tf_op jit(solution)/shard_map/slice | solution.py:107
  7.5 0.4 %collective-permute-start.3 = (bf16[8,8192]{1,0:T(8,128)(2,1)S(1)}, bf16[8,8192]{1,0:T(8,128)(2,1)S(1)}, u32[]{:S(2)}, u32[]{:S(2)}) collective-permute-start(bf16[8,8192]{1,0:T(8,128)(2,1)S(1)} %slice.7.refs_1_), channel_id=1, source_target_pairs={{0,2},{1,3},{2,0},{3,1},{4,6},{5,7},{6,4},{7,5},{8,10},{9,11},{10,... | collective-permute-start | bytes 393224 | tf_op jit(solution)/shard_map/ppermute | solution.py:91
  7.9 0.2 collective-permute-start.2
  8.1 3.7 %collective-permute-done = bf16[8,8192]{1,0:T(8,128)(2,1)S(1)} collective-permute-done((bf16[8,8192]{1,0:T(8,128)(2,1)S(1)}, bf16[8,8192]{1,0:T(8,128)(2,1)S(1)}, u32[]{:S(2)}, u32[]{:S(2)}) %collective-permute-start) | collective-permute-done | bytes 131104 | tf_op jit(solution)/shard_map/ppermute | solution.py:117
  11.9 0.0 collective-permute-done.1
  11.9 4.0 %collective-permute-start.4 = (bf16[8,8192]{1,0:T(8,128)(2,1)S(1)}, bf16[8,8192]{1,0:T(8,128)(2,1)S(1)}, u32[]{:S(2)}, u32[]{:S(2)}) collective-permute-start(bf16[8,8192]{1,0:T(8,128)(2,1)S(1)} %get-tuple-element.23.refs_2_), channel_id=1, source_target_pairs={{0,1},{1,0},{2,3},{3,2},{4,5},{5,4},{6,7},{7,6},{8,9},{9,8},{10,11... | collective-permute-start | bytes 393224 | tf_op jit(solution)/shard_map/ppermute | solution.py:91
  15.9 1.5 %collective-permute-done.3.refs_3_ = bf16[8,8192]{1,0:T(8,128)(2,1)S(1)} collective-permute-done((bf16[8,8192]{1,0:T(8,128)(2,1)S(1)}, bf16[8,8192]{1,0:T(8,128)(2,1)S(1)}, u32[]{:S(2)}, u32[]{:S(2)}) %collective-permute-start.3) | collective-permute-done | bytes 131104 | tf_op jit(solution)/shard_map/ppermute | solution.py:91
  17.4 0.6 %collective-permute-start.5 = (bf16[8,8192]{1,0:T(8,128)(2,1)S(1)}, bf16[8,8192]{1,0:T(8,128)(2,1)S(1)}, u32[]{:S(2)}, u32[]{:S(2)}) collective-permute-start(bf16[8,8192]{1,0:T(8,128)(2,1)S(1)} %collective-permute-done.3.refs_3_), channel_id=1, source_target_pairs={{0,1},{1,0},{2,3},{3,2},{4,5},{5,4},{6,7},{7,6},{8,9},{9,8},{10,11... | collective-permute-start | bytes 393224 | tf_op jit(solution)/shard_map/ppermute | solution.py:91
  18.7 0.0 copy-start
  18.7 1.6 %copy-done = bf16[64,16384]{1,0:T(8,128)(2,1)S(1)} copy-done((bf16[64,16384]{1,0:T(8,128)(2,1)S(1)}, bf16[64,16384]{1,0:T(8,128)(2,1)}, u32[]{:S(2)}) %copy-start) | copy-done | bytes 2097176
  20.3 0.0 copy-start.1
  20.3 0.8 %copy-done.1 = f32[16384]{0:T(1024)S(1)} copy-done((f32[16384]{0:T(1024)S(1)}, f32[16384]{0:T(1024)}, u32[]{:S(2)}) %copy-start.1) | copy-done | bytes 65560
  21.1 0.6 %shard_map.46 = (f32[8,64]{1,0:T(8,128)S(1)}, f32[1,16384]{1,0:T(1,128)S(1)}) custom-call(bf16[64,16384]{1,0:T(8,128)(2,1)S(1)} %copy-done, f32[1,16384]{1,0:T(1,128)S(1)} %bitcast.1, bf16[8,8192]{1,0:T(8,128)(2,1)S(1)} %slice.6.refs_0_, bf16[8,8192]{1,0:T(8,128)(2,1)S(1)} %slice.7.refs_1_), custom_call_target="tpu_custom_call" | custom-call | tf_op jit(solution)/shard_map/pallas_call | solution.py:94
  21.7 0.0 collective-permute-done.2.refs_1_
  21.7 1.2 %shard_map.47 = (f32[8,64]{1,0:T(8,128)S(1)}, f32[8,64]{1,0:T(8,128)S(1)}) custom-call(bf16[64,16384]{1,0:T(8,128)(2,1)S(1)} %copy-done, f32[1,16384]{1,0:T(1,128)S(1)} %get-tuple-element.15.gain_ref, bf16[8,8192]{1,0:T(8,128)(2,1)S(1)} %get-tuple-element.24.refs_0_, bf16[8,8192]{1,0:T(8,128)(2,1)S(1)} %collective-permute-done.2.refs_1_, ...), custom_call_target="tpu_custom_call" | custom-call | tf_op jit(solution)/shard_map/pallas_call | solution.py:94
  22.9 0.0 collective-permute-done.4.refs_0_
  22.9 0.4 %shard_map.48.cross = f32[8,64]{1,0:T(8,128)S(1)} custom-call(bf16[64,16384]{1,0:T(8,128)(2,1)S(1)} %copy-done, f32[1,16384]{1,0:T(1,128)S(1)} %get-tuple-element.15.gain_ref, bf16[8,8192]{1,0:T(8,128)(2,1)S(1)} %collective-permute-done.4.refs_0_), custom_call_target="tpu_custom_call" | custom-call | tf_op jit(solution)/shard_map/pallas_call | solution.py:94
  23.3 0.1 collective-permute-done.5.final
  23.4 0.5 %shard_map.49 = (f32[16,32]{1,0:T(8,128)S(1)}, f32[16,32]{1,0:T(8,128)S(1)}, f32[16,32]{1,0:T(8,128)S(1)}, f32[16,32]{1,0:T(8,128)S(1)}) custom-call(s32[1]{0:T(128)S(6)} %copy.5.count_ref, bf16[64,16384]{1,0:T(8,128)(2,1)S(1)} %copy-done, f32[1,16384]{1,0:T(1,128)S(1)} %get-tuple-element.15.gain_ref, f32[8,64]{1,0:T(8,128)S(1)} %get-tuple-element.16.own, ...), custom_call_target="tpu_custom_call" | custom-call | tf_op jit(solution)/shard_map/pallas_call | solution.py:94
  23.9 0.1 collective-permute-start.6
  24.0 1.9 %collective-permute-start.7 = (f32[16,32]{1,0:T(8,128)S(1)}, f32[16,32]{1,0:T(8,128)S(1)}, u32[]{:S(2)}, u32[]{:S(2)}) collective-permute-start(f32[16,32]{1,0:T(8,128)S(1)} %get-tuple-element.21), channel_id=1, source_target_pairs={{0,8},{4,12},{8,0},{12,4},{1,9},{5,13},{9,1},{13,5},{2,10},{6,14},... | collective-permute-start | bytes 6152 | tf_op jit(solution)/shard_map/ppermute | solution.py:91
  25.9 0.0 collective-permute-start.8
  25.9 0.0 collective-permute-done.6
  25.9 1.8 %collective-permute-done.7 = f32[16,32]{1,0:T(8,128)S(1)} collective-permute-done((f32[16,32]{1,0:T(8,128)S(1)}, f32[16,32]{1,0:T(8,128)S(1)}, u32[]{:S(2)}, u32[]{:S(2)}) %collective-permute-start.7) | collective-permute-done | bytes 2080 | tf_op jit(solution)/shard_map/ppermute | solution.py:91
  27.7 1.2 %collective-permute-done.8 = f32[16,32]{1,0:T(8,128)S(1)} collective-permute-done((f32[16,32]{1,0:T(8,128)S(1)}, f32[16,32]{1,0:T(8,128)S(1)}, u32[]{:S(2)}, u32[]{:S(2)}) %collective-permute-start.8) | collective-permute-done | bytes 2080 | tf_op jit(solution)/shard_map/ppermute | solution.py:91
  29.0 0.6 %add_add_fusion = f32[16,32]{1,0:T(8,128)} fusion(f32[16,32]{1,0:T(8,128)S(1)} %collective-permute-done.8, f32[16,32]{1,0:T(8,128)S(1)} %collective-permute-done.7, f32[16,32]{1,0:T(8,128)S(1)} %get-tuple-element.19, f32[16,32]{1,0:T(8,128)S(1)} %collective-permute-done.6), kind=kLoop, calls=%fused_computation.2 | loop fusion | flops 1536 | bytes 10240 | tf_op jit(solution)/shard_map/add | solution.py:147
  (1 shorter events, 0.0 us)
Async XLA Ops:
  0.9 11.0 %collective-permute-start = (bf16[8,8192]{1,0:T(8,128)(2,1)S(1)}, bf16[8,8192]{1,0:T(8,128)(2,1)S(1)}, u32[]{:S(2)}, u32[]{:S(2)}) collective-permute-start(bf16[8,8192]{1,0:T(8,128)(2,1)S(1)} %slice.6.refs_0_), channel_id=1, source_target_pairs={{0,2},{1,3},{2,0},{3,1},{4,5},{5,4},{6,7},{7,6},{8,10},{9,11},{10,... | collective-permute-start | bytes 393224 | tf_op jit(solution)/shard_map/ppermute | solution.py:117
  5.0 6.8 %collective-permute-start.1 = (bf16[8,8192]{1,0:T(8,128)(2,1)S(1)}, bf16[8,8192]{1,0:T(8,128)(2,1)S(1)}, u32[]{:S(2)}, u32[]{:S(2)}) collective-permute-start(bf16[8,8192]{1,0:T(8,128)(2,1)S(1)} %slice.6.refs_0_), channel_id=1, source_target_pairs={{0,1},{1,0},{2,3},{3,2},{4,6},{5,7},{6,4},{7,5},{8,9},{9,8},{10,11... | collective-permute-start | bytes 393224 | tf_op jit(solution)/shard_map/ppermute | solution.py:117
  7.5 9.9 %collective-permute-start.3 = (bf16[8,8192]{1,0:T(8,128)(2,1)S(1)}, bf16[8,8192]{1,0:T(8,128)(2,1)S(1)}, u32[]{:S(2)}, u32[]{:S(2)}) collective-permute-start(bf16[8,8192]{1,0:T(8,128)(2,1)S(1)} %slice.7.refs_1_), channel_id=1, source_target_pairs={{0,2},{1,3},{2,0},{3,1},{4,6},{5,7},{6,4},{7,5},{8,10},{9,11},{10,... | collective-permute-start | bytes 393224 | tf_op jit(solution)/shard_map/ppermute | solution.py:91
  7.9 13.8 %collective-permute-start.2 = (bf16[8,8192]{1,0:T(8,128)(2,1)S(1)}, bf16[8,8192]{1,0:T(8,128)(2,1)S(1)}, u32[]{:S(2)}, u32[]{:S(2)}) collective-permute-start(bf16[8,8192]{1,0:T(8,128)(2,1)S(1)} %slice.7.refs_1_), channel_id=1, source_target_pairs={{0,1},{1,0},{2,3},{3,2},{4,5},{5,4},{6,7},{7,6},{8,9},{9,8},{10,11... | collective-permute-start | bytes 393224 | tf_op jit(solution)/shard_map/ppermute | solution.py:91
  11.9 11.0 %collective-permute-start.4 = (bf16[8,8192]{1,0:T(8,128)(2,1)S(1)}, bf16[8,8192]{1,0:T(8,128)(2,1)S(1)}, u32[]{:S(2)}, u32[]{:S(2)}) collective-permute-start(bf16[8,8192]{1,0:T(8,128)(2,1)S(1)} %get-tuple-element.23.refs_2_), channel_id=1, source_target_pairs={{0,1},{1,0},{2,3},{3,2},{4,5},{5,4},{6,7},{7,6},{8,9},{9,8},{10,11... | collective-permute-start | bytes 393224 | tf_op jit(solution)/shard_map/ppermute | solution.py:91
  17.4 6.0 %collective-permute-start.5 = (bf16[8,8192]{1,0:T(8,128)(2,1)S(1)}, bf16[8,8192]{1,0:T(8,128)(2,1)S(1)}, u32[]{:S(2)}, u32[]{:S(2)}) collective-permute-start(bf16[8,8192]{1,0:T(8,128)(2,1)S(1)} %collective-permute-done.3.refs_3_), channel_id=1, source_target_pairs={{0,1},{1,0},{2,3},{3,2},{4,5},{5,4},{6,7},{7,6},{8,9},{9,8},{10,11... | collective-permute-start | bytes 393224 | tf_op jit(solution)/shard_map/ppermute | solution.py:91
  18.7 1.6 %copy-start = (bf16[64,16384]{1,0:T(8,128)(2,1)S(1)}, bf16[64,16384]{1,0:T(8,128)(2,1)}, u32[]{:S(2)}) copy-start(bf16[64,16384]{1,0:T(8,128)(2,1)} %train_ref.7) | copy-start | bytes 6291460
  20.3 0.8 %copy-start.1 = (f32[16384]{0:T(1024)S(1)}, f32[16384]{0:T(1024)}, u32[]{:S(2)}) copy-start(f32[16384]{0:T(1024)} %param.6) | copy-start | bytes 196612
  23.9 2.0 %collective-permute-start.6 = (f32[16,32]{1,0:T(8,128)S(1)}, f32[16,32]{1,0:T(8,128)S(1)}, u32[]{:S(2)}, u32[]{:S(2)}) collective-permute-start(f32[16,32]{1,0:T(8,128)S(1)} %get-tuple-element.20), channel_id=1, source_target_pairs={{0,4},{4,0},{8,12},{12,8},{1,5},{5,1},{9,13},{13,9},{2,6},{6,2},{1... | collective-permute-start | bytes 6152 | tf_op jit(solution)/shard_map/ppermute | solution.py:91
  24.0 3.7 %collective-permute-start.7 = (f32[16,32]{1,0:T(8,128)S(1)}, f32[16,32]{1,0:T(8,128)S(1)}, u32[]{:S(2)}, u32[]{:S(2)}) collective-permute-start(f32[16,32]{1,0:T(8,128)S(1)} %get-tuple-element.21), channel_id=1, source_target_pairs={{0,8},{4,12},{8,0},{12,4},{1,9},{5,13},{9,1},{13,5},{2,10},{6,14},... | collective-permute-start | bytes 6152 | tf_op jit(solution)/shard_map/ppermute | solution.py:91
  25.9 3.1 %collective-permute-start.8 = (f32[16,32]{1,0:T(8,128)S(1)}, f32[16,32]{1,0:T(8,128)S(1)}, u32[]{:S(2)}, u32[]{:S(2)}) collective-permute-start(f32[16,32]{1,0:T(8,128)S(1)} %get-tuple-element.22), channel_id=1, source_target_pairs={{0,12},{4,8},{8,4},{12,0},{1,13},{5,9},{9,5},{13,1},{2,14},{6,10},... | collective-permute-start | bytes 6152 | tf_op jit(solution)/shard_map/ppermute | solution.py:91

commit v5 on v4

--- a/solution.py
+++ b/solution.py
@@ -121,8 +121,10 @@
     second = turns(chunks[0], 2, 1)
     pick = lambda on_odd, on_even: jnp.where(odd, on_odd, on_even)
     far0, near0 = pick(first, second), pick(second, first)
-    far = [far0] + [swap(chunk, "loop", 2) for k, chunk in enumerate(chunks) if k]
-    near = [near0] + [swap(chunk, "loop", 1) for k, chunk in enumerate(chunks) if k]
+    third = turns(chunks[1], 2, 1)
+    fourth = turns(chunks[1], 1, 2)
+    far1, near1 = pick(fourth, third), pick(third, fourth)
+    far, near = [far0, far1], [near0, near1]
     own_score, gain = kernel(
         own_kernel,
         [score, jax.ShapeDtypeStruct((1, features), jnp.float32)],

time: 29.8 us -> 31.2 us (1.047)
  waiting for transfers between devices: 8.4 us -> 10.1 us
    ppermute x2 -> x4, waiting for transfers between devices: 3.74 us -> 7.31 us  [turns(): return lax.ppermute(piece, ('feat', 'loop'), pairs)]
    ppermute x7 -> x5, waiting for transfers between devices: 4.66 us -> 2.79 us  [swap(): return lax.ppermute(piece, axis, pairs)]
    ppermute x7 -> x5, starting transfers between devices: 7.18 us -> 6.28 us  [swap(): return lax.ppermute(piece, axis, pairs)]
    ppermute x2 -> x4, starting transfers between devices: 5.71 us -> 6.3 us  [turns(): return lax.ppermute(piece, ('feat', 'loop'), pairs)]
  transfers between devices with their start and end apart: 9 -> 9, of which waited for: 5 -> 4; matrix products, arithmetic and copies ran while one was open for 3% -> 3% of each run, Pallas kernels for 8% -> 7%
where the time goes in v5:
time: 31.2 us; the launch traced here: 31 us
  starting transfers between devices  12.6 us (40%)
  waiting for transfers between devices  10.1 us (32%)
  local copies, waits for them, and re-layouts  4.25 us (14%)
  Pallas kernels  2.74 us (9%)
  between operations  0.7 us (2%)
  other arithmetic  0.65 us (2%)
    ppermute x4, waiting for transfers between devices, turns(): return lax.ppermute(piece, ('feat', 'loop'), pairs)  7.31 us
    ppermute x4, starting transfers between devices, turns(): return lax.ppermute(piece, ('feat', 'loop'), pairs)  6.3 us
    ppermute x5, starting transfers between devices, swap(): return lax.ppermute(piece, axis, pairs)  6.28 us
    ppermute x5, waiting for transfers between devices, swap(): return lax.ppermute(piece, axis, pairs)  2.79 us
    pallas_call x4, Pallas kernels, kernel(): pl.pallas_call(body, out_shape=shapes, in_specs=[smem] * smems + [vmem] *...  2.74 us
    unnamed x4, local copies, waits for them, and re-layouts  2.43 us
    slice x2, local copies, waits for them, and re-layouts, permuted(): chunks.append(after[:, start:end])  1.83 us
  transfers between devices with their start and end apart: 9, of which 4 were waited for; matrix products, arithmetic and copies ran while one was open for 3% of the time, Pallas kernels for 7%

profile of v5, /device:TPU:0, one launch (start us, length us, event | category | flops | bytes accessed | tf_op | source)
XLA Modules:
  0.0 31.0 jit_solution(486087574435534921)
XLA Ops:
  0.0 0.9 %slice.6.refs_0_ = bf16[8,8192]{1,0:T(8,128)(2,1)S(1)} slice(bf16[8,16384]{1,0:T(8,128)(2,1)} %param.5), slice={[0:8], [0:8192]} | slice | bytes 262144 | tf_op jit(solution)/shard_map/slice | solution.py:107
  0.9 4.1 %collective-permute-start = (bf16[8,8192]{1,0:T(8,128)(2,1)S(1)}, bf16[8,8192]{1,0:T(8,128)(2,1)S(1)}, u32[]{:S(2)}, u32[]{:S(2)}) collective-permute-start(bf16[8,8192]{1,0:T(8,128)(2,1)S(1)} %slice.6.refs_0_), channel_id=1, source_target_pairs={{0,2},{1,3},{2,0},{3,1},{4,5},{5,4},{6,7},{7,6},{8,10},{9,11},{10,... | collective-permute-start | bytes 393224 | tf_op jit(solution)/shard_map/ppermute | solution.py:117
  5.0 1.6 %collective-permute-start.1 = (bf16[8,8192]{1,0:T(8,128)(2,1)S(1)}, bf16[8,8192]{1,0:T(8,128)(2,1)S(1)}, u32[]{:S(2)}, u32[]{:S(2)}) collective-permute-start(bf16[8,8192]{1,0:T(8,128)(2,1)S(1)} %slice.6.refs_0_), channel_id=1, source_target_pairs={{0,1},{1,0},{2,3},{3,2},{4,6},{5,7},{6,4},{7,5},{8,9},{9,8},{10,11... | collective-permute-start | bytes 393224 | tf_op jit(solution)/shard_map/ppermute | solution.py:117
  6.6 0.9 %slice.7.refs_1_ = bf16[8,8192]{1,0:T(8,128)(2,1)S(1)} slice(bf16[8,16384]{1,0:T(8,128)(2,1)} %param.5), slice={[0:8], [8192:16384]} | slice | bytes 262144 | tf_op jit(solution)/shard_map/slice | solution.py:107
  7.5 0.4 %collective-permute-start.2 = (bf16[8,8192]{1,0:T(8,128)(2,1)S(1)}, bf16[8,8192]{1,0:T(8,128)(2,1)S(1)}, u32[]{:S(2)}, u32[]{:S(2)}) collective-permute-start(bf16[8,8192]{1,0:T(8,128)(2,1)S(1)} %slice.7.refs_1_), channel_id=1, source_target_pairs={{0,2},{1,3},{2,0},{3,1},{4,5},{5,4},{6,7},{7,6},{8,10},{9,11},{10,... | collective-permute-start | bytes 393224 | tf_op jit(solution)/shard_map/ppermute | solution.py:117
  7.9 0.2 collective-permute-start.3
  8.1 3.7 %collective-permute-done = bf16[8,8192]{1,0:T(8,128)(2,1)S(1)} collective-permute-done((bf16[8,8192]{1,0:T(8,128)(2,1)S(1)}, bf16[8,8192]{1,0:T(8,128)(2,1)S(1)}, u32[]{:S(2)}, u32[]{:S(2)}) %collective-permute-start) | collective-permute-done | bytes 131104 | tf_op jit(solution)/shard_map/ppermute | solution.py:117
  11.8 0.0 collective-permute-done.1
  11.8 2.4 %collective-permute-start.4 = (bf16[8,8192]{1,0:T(8,128)(2,1)S(1)}, bf16[8,8192]{1,0:T(8,128)(2,1)S(1)}, u32[]{:S(2)}, u32[]{:S(2)}) collective-permute-start(bf16[8,8192]{1,0:T(8,128)(2,1)S(1)} %get-tuple-element.25.refs_2_), channel_id=1, source_target_pairs={{0,1},{1,0},{2,3},{3,2},{4,5},{5,4},{6,7},{7,6},{8,9},{9,8},{10,11... | collective-permute-start | bytes 393224 | tf_op jit(solution)/shard_map/ppermute | solution.py:91
  14.2 3.6 %collective-permute-done.2 = bf16[8,8192]{1,0:T(8,128)(2,1)S(1)} collective-permute-done((bf16[8,8192]{1,0:T(8,128)(2,1)S(1)}, bf16[8,8192]{1,0:T(8,128)(2,1)S(1)}, u32[]{:S(2)}, u32[]{:S(2)}) %collective-permute-start.2) | collective-permute-done | bytes 131104 | tf_op jit(solution)/shard_map/ppermute | solution.py:117
  17.8 0.0 collective-permute-done.3
  17.9 2.0 %collective-permute-start.5 = (bf16[8,8192]{1,0:T(8,128)(2,1)S(1)}, bf16[8,8192]{1,0:T(8,128)(2,1)S(1)}, u32[]{:S(2)}, u32[]{:S(2)}) collective-permute-start(bf16[8,8192]{1,0:T(8,128)(2,1)S(1)} %get-tuple-element.23.refs_3_), channel_id=1, source_target_pairs={{0,1},{1,0},{2,3},{3,2},{4,5},{5,4},{6,7},{7,6},{8,9},{9,8},{10,11... | collective-permute-start | bytes 393224 | tf_op jit(solution)/shard_map/ppermute | solution.py:91
  20.5 0.0 copy-start
  20.5 1.6 %copy-done = bf16[64,16384]{1,0:T(8,128)(2,1)S(1)} copy-done((bf16[64,16384]{1,0:T(8,128)(2,1)S(1)}, bf16[64,16384]{1,0:T(8,128)(2,1)}, u32[]{:S(2)}) %copy-start) | copy-done | bytes 2097176
  22.1 0.0 copy-start.1
  22.1 0.8 %copy-done.1 = f32[16384]{0:T(1024)S(1)} copy-done((f32[16384]{0:T(1024)S(1)}, f32[16384]{0:T(1024)}, u32[]{:S(2)}) %copy-start.1) | copy-done | bytes 65560
  23.0 0.6 %shard_map.46 = (f32[8,64]{1,0:T(8,128)S(1)}, f32[1,16384]{1,0:T(1,128)S(1)}) custom-call(bf16[64,16384]{1,0:T(8,128)(2,1)S(1)} %copy-done, f32[1,16384]{1,0:T(1,128)S(1)} %bitcast.1, bf16[8,8192]{1,0:T(8,128)(2,1)S(1)} %slice.6.refs_0_, bf16[8,8192]{1,0:T(8,128)(2,1)S(1)} %slice.7.refs_1_), custom_call_target="tpu_custom_call" | custom-call | tf_op jit(solution)/shard_map/pallas_call | solution.py:94
  23.6 1.2 %shard_map.47 = (f32[8,64]{1,0:T(8,128)S(1)}, f32[8,64]{1,0:T(8,128)S(1)}) custom-call(bf16[64,16384]{1,0:T(8,128)(2,1)S(1)} %copy-done, f32[1,16384]{1,0:T(1,128)S(1)} %get-tuple-element.15.gain_ref, bf16[8,8192]{1,0:T(8,128)(2,1)S(1)} %get-tuple-element.26.refs_0_, bf16[8,8192]{1,0:T(8,128)(2,1)S(1)} %get-tuple-element.24.refs_1_, ...), custom_call_target="tpu_custom_call" | custom-call | tf_op jit(solution)/shard_map/pallas_call | solution.py:94
  24.8 0.0 collective-permute-done.4.refs_0_
  24.8 0.4 %shard_map.48.cross = f32[8,64]{1,0:T(8,128)S(1)} custom-call(bf16[64,16384]{1,0:T(8,128)(2,1)S(1)} %copy-done, f32[1,16384]{1,0:T(1,128)S(1)} %get-tuple-element.15.gain_ref, bf16[8,8192]{1,0:T(8,128)(2,1)S(1)} %collective-permute-done.4.refs_0_), custom_call_target="tpu_custom_call" | custom-call | tf_op jit(solution)/shard_map/pallas_call | solution.py:94
  25.2 0.0 collective-permute-done.5.final
  25.2 0.5 %shard_map.49 = (f32[16,32]{1,0:T(8,128)S(1)}, f32[16,32]{1,0:T(8,128)S(1)}, f32[16,32]{1,0:T(8,128)S(1)}, f32[16,32]{1,0:T(8,128)S(1)}) custom-call(s32[1]{0:T(128)S(6)} %copy.5.count_ref, bf16[64,16384]{1,0:T(8,128)(2,1)S(1)} %copy-done, f32[1,16384]{1,0:T(1,128)S(1)} %get-tuple-element.15.gain_ref, f32[8,64]{1,0:T(8,128)S(1)} %get-tuple-element.16.own, ...), custom_call_target="tpu_custom_call" | custom-call | tf_op jit(solution)/shard_map/pallas_call | solution.py:94
  25.7 0.1 collective-permute-start.6
  25.8 1.6 %collective-permute-start.7 = (f32[16,32]{1,0:T(8,128)S(1)}, f32[16,32]{1,0:T(8,128)S(1)}, u32[]{:S(2)}, u32[]{:S(2)}) collective-permute-start(f32[16,32]{1,0:T(8,128)S(1)} %get-tuple-element.21), channel_id=1, source_target_pairs={{0,8},{4,12},{8,0},{12,4},{1,9},{5,13},{9,1},{13,5},{2,10},{6,14},... | collective-permute-start | bytes 6152 | tf_op jit(solution)/shard_map/ppermute | solution.py:91
  27.3 0.3 collective-permute-start.8
  27.6 0.0 collective-permute-done.6
  27.6 1.9 %collective-permute-done.7 = f32[16,32]{1,0:T(8,128)S(1)} collective-permute-done((f32[16,32]{1,0:T(8,128)S(1)}, f32[16,32]{1,0:T(8,128)S(1)}, u32[]{:S(2)}, u32[]{:S(2)}) %collective-permute-start.7) | collective-permute-done | bytes 2080 | tf_op jit(solution)/shard_map/ppermute | solution.py:91
  29.5 0.9 %collective-permute-done.8 = f32[16,32]{1,0:T(8,128)S(1)} collective-permute-done((f32[16,32]{1,0:T(8,128)S(1)}, f32[16,32]{1,0:T(8,128)S(1)}, u32[]{:S(2)}, u32[]{:S(2)}) %collective-permute-start.8) | collective-permute-done | bytes 2080 | tf_op jit(solution)/shard_map/ppermute | solution.py:91
  30.4 0.6 %add_add_fusion = f32[16,32]{1,0:T(8,128)} fusion(f32[16,32]{1,0:T(8,128)S(1)} %collective-permute-done.8, f32[16,32]{1,0:T(8,128)S(1)} %collective-permute-done.7, f32[16,32]{1,0:T(8,128)S(1)} %get-tuple-element.19, f32[16,32]{1,0:T(8,128)S(1)} %collective-permute-done.6), kind=kLoop, calls=%fused_computation.4 | loop fusion | flops 1536 | bytes 10240 | tf_op jit(solution)/shard_map/add | solution.py:149
  (2 shorter events, 0.0 us)
Async XLA Ops:
  0.9 10.9 %collective-permute-start = (bf16[8,8192]{1,0:T(8,128)(2,1)S(1)}, bf16[8,8192]{1,0:T(8,128)(2,1)S(1)}, u32[]{:S(2)}, u32[]{:S(2)}) collective-permute-start(bf16[8,8192]{1,0:T(8,128)(2,1)S(1)} %slice.6.refs_0_), channel_id=1, source_target_pairs={{0,2},{1,3},{2,0},{3,1},{4,5},{5,4},{6,7},{7,6},{8,10},{9,11},{10,... | collective-permute-start | bytes 393224 | tf_op jit(solution)/shard_map/ppermute | solution.py:117
  5.0 6.8 %collective-permute-start.1 = (bf16[8,8192]{1,0:T(8,128)(2,1)S(1)}, bf16[8,8192]{1,0:T(8,128)(2,1)S(1)}, u32[]{:S(2)}, u32[]{:S(2)}) collective-permute-start(bf16[8,8192]{1,0:T(8,128)(2,1)S(1)} %slice.6.refs_0_), channel_id=1, source_target_pairs={{0,1},{1,0},{2,3},{3,2},{4,6},{5,7},{6,4},{7,5},{8,9},{9,8},{10,11... | collective-permute-start | bytes 393224 | tf_op jit(solution)/shard_map/ppermute | solution.py:117
  7.5 10.3 %collective-permute-start.2 = (bf16[8,8192]{1,0:T(8,128)(2,1)S(1)}, bf16[8,8192]{1,0:T(8,128)(2,1)S(1)}, u32[]{:S(2)}, u32[]{:S(2)}) collective-permute-start(bf16[8,8192]{1,0:T(8,128)(2,1)S(1)} %slice.7.refs_1_), channel_id=1, source_target_pairs={{0,2},{1,3},{2,0},{3,1},{4,5},{5,4},{6,7},{7,6},{8,10},{9,11},{10,... | collective-permute-start | bytes 393224 | tf_op jit(solution)/shard_map/ppermute | solution.py:117
  7.9 9.9 %collective-permute-start.3 = (bf16[8,8192]{1,0:T(8,128)(2,1)S(1)}, bf16[8,8192]{1,0:T(8,128)(2,1)S(1)}, u32[]{:S(2)}, u32[]{:S(2)}) collective-permute-start(bf16[8,8192]{1,0:T(8,128)(2,1)S(1)} %slice.7.refs_1_), channel_id=1, source_target_pairs={{0,1},{1,0},{2,3},{3,2},{4,6},{5,7},{6,4},{7,5},{8,9},{9,8},{10,11... | collective-permute-start | bytes 393224 | tf_op jit(solution)/shard_map/ppermute | solution.py:117
  11.8 12.9 %collective-permute-start.4 = (bf16[8,8192]{1,0:T(8,128)(2,1)S(1)}, bf16[8,8192]{1,0:T(8,128)(2,1)S(1)}, u32[]{:S(2)}, u32[]{:S(2)}) collective-permute-start(bf16[8,8192]{1,0:T(8,128)(2,1)S(1)} %get-tuple-element.25.refs_2_), channel_id=1, source_target_pairs={{0,1},{1,0},{2,3},{3,2},{4,5},{5,4},{6,7},{7,6},{8,9},{9,8},{10,11... | collective-permute-start | bytes 393224 | tf_op jit(solution)/shard_map/ppermute | solution.py:91
  17.9 7.3 %collective-permute-start.5 = (bf16[8,8192]{1,0:T(8,128)(2,1)S(1)}, bf16[8,8192]{1,0:T(8,128)(2,1)S(1)}, u32[]{:S(2)}, u32[]{:S(2)}) collective-permute-start(bf16[8,8192]{1,0:T(8,128)(2,1)S(1)} %get-tuple-element.23.refs_3_), channel_id=1, source_target_pairs={{0,1},{1,0},{2,3},{3,2},{4,5},{5,4},{6,7},{7,6},{8,9},{9,8},{10,11... | collective-permute-start | bytes 393224 | tf_op jit(solution)/shard_map/ppermute | solution.py:91
  20.5 1.6 %copy-start = (bf16[64,16384]{1,0:T(8,128)(2,1)S(1)}, bf16[64,16384]{1,0:T(8,128)(2,1)}, u32[]{:S(2)}) copy-start(bf16[64,16384]{1,0:T(8,128)(2,1)} %train_ref.7) | copy-start | bytes 6291460
  22.1 0.8 %copy-start.1 = (f32[16384]{0:T(1024)S(1)}, f32[16384]{0:T(1024)}, u32[]{:S(2)}) copy-start(f32[16384]{0:T(1024)} %param.6) | copy-start | bytes 196612
  25.7 1.9 %collective-permute-start.6 = (f32[16,32]{1,0:T(8,128)S(1)}, f32[16,32]{1,0:T(8,128)S(1)}, u32[]{:S(2)}, u32[]{:S(2)}) collective-permute-start(f32[16,32]{1,0:T(8,128)S(1)} %get-tuple-element.20), channel_id=1, source_target_pairs={{0,4},{4,0},{8,12},{12,8},{1,5},{5,1},{9,13},{13,9},{2,6},{6,2},{1... | collective-permute-start | bytes 6152 | tf_op jit(solution)/shard_map/ppermute | solution.py:91
  25.8 3.7 %collective-permute-start.7 = (f32[16,32]{1,0:T(8,128)S(1)}, f32[16,32]{1,0:T(8,128)S(1)}, u32[]{:S(2)}, u32[]{:S(2)}) collective-permute-start(f32[16,32]{1,0:T(8,128)S(1)} %get-tuple-element.21), channel_id=1, source_target_pairs={{0,8},{4,12},{8,0},{12,4},{1,9},{5,13},{9,1},{13,5},{2,10},{6,14},... | collective-permute-start | bytes 6152 | tf_op jit(solution)/shard_map/ppermute | solution.py:91
  27.3 3.1 %collective-permute-start.8 = (f32[16,32]{1,0:T(8,128)S(1)}, f32[16,32]{1,0:T(8,128)S(1)}, u32[]{:S(2)}, u32[]{:S(2)}) collective-permute-start(f32[16,32]{1,0:T(8,128)S(1)} %get-tuple-element.22), channel_id=1, source_target_pairs={{0,12},{4,8},{8,4},{12,0},{1,13},{5,9},{9,5},{13,1},{2,14},{6,10},... | collective-permute-start | bytes 6152 | tf_op jit(solution)/shard_map/ppermute | solution.py:91
